TPU v7x, 256 devices: a whole 4x4x8 slice. The times are simulated.
256 devices in a mesh: mats: 64 (over z, x, core), tp: 4 (over y).
Axes of the slice: x: 4, y: 4, z: 8, core: 2. Of those that a mesh axis runs over, the one named last changes fastest.
Arguments:
- grad: bfloat16 [3072, 16384], P('tp', 'mats'), may hold values from -40 to 40
- momentum: float32 [3072, 16384], P('tp', 'mats'), may hold values from -6 to 6
Outputs:
- update: bfloat16 [3072, 16384], P('tp', 'mats')
- new_momentum: float32 [3072, 16384], P('tp', 'mats')
All inputs are finite; a program needn't handle non-finite values.
Results may differ from a plain program's by a relative error of at most 0.01.
Values may be sent and summed in bfloat16 or wider, within the bound.
A program may use at most 64 MiB of HBM per device.

v0:
```python
import math

import jax
import jax.numpy as jnp
from jax import lax
from jax.sharding import Mesh
from jax.sharding import PartitionSpec as P

R = 3072
C = 16384
ITERS = 2
MATS = ("mats_0", "mats_1", "mats_2")


momentum_beta = 0.95
first_coef = 3.4445
second_coef = -4.775
third_coef = 2.0315
shape_gain = 0.2
epsilon = 1e-06


def laid_out(tiles, dim):
    tiles = jnp.moveaxis(tiles, 0, dim)
    lengths = tiles.shape
    return tiles.reshape(*lengths[:dim], lengths[dim] * lengths[dim + 1], *lengths[dim + 2 :])


def sent_to_all(array, axis):
    copies = jnp.broadcast_to(array, (lax.axis_size(axis), *array.shape))
    return lax.all_to_all(copies, axis, split_axis=0, concat_axis=0, tiled=True)


def gather_directly(array, axis, dim):
    return laid_out(sent_to_all(array, axis), dim)


def gather_in_order(array, axes, sequence):
    tiles = array[None]
    for k in sequence:
        tiles = lax.all_gather(tiles, axes[k], axis=0, tiled=True)
    block = [lax.axis_size(axes[k]) for k in reversed(sequence)]
    tiles = tiles.reshape(*block, *array.shape)
    turned = sorted(range(len(sequence)), key=lambda place: sequence[len(sequence) - 1 - place])
    return tiles.transpose(*turned, *range(len(sequence), tiles.ndim)).reshape(-1, *array.shape)


def whole_of(array, axes, sequence, dim):
    return laid_out(gather_in_order(array, axes, sequence), dim)


def over_copies(array, axis):
    everything = sent_to_all(array, axis)
    return jnp.sum(everything, axis=0)


def taken_together(array, axis):
    everything = sent_to_all(array, axis)
    return jnp.max(everything, axis=0)


def row_dot(left, right):
    return lax.dot_general(
        left, right, (((1,), (1,)), ((), ())), preferred_element_type=jnp.float32
    )


def per_device(grad, momentum):
    new_momentum = momentum_beta * momentum + grad.astype(jnp.float32)
    iterate = (grad.astype(jnp.float32) + momentum_beta * new_momentum).astype(jnp.bfloat16)
    for step in range(ITERS):
        columns = gather_directly(iterate, "tp", 0)
        partial_gram = row_dot(iterate, columns)
        share = lax.psum_scatter(partial_gram, MATS, scatter_dimension=1, tiled=True).astype(
            jnp.bfloat16
        )
        gram = whole_of(share, MATS, (1, 0, 2), 1)
        if step == 0:
            share_sums = jnp.sum(jnp.abs(share.astype(jnp.float32)), axis=1)
            row_sums = over_copies(share_sums, MATS)
            bound = taken_together(jnp.max(row_sums), "tp") + epsilon
            root = lax.rsqrt(bound)
        first = jnp.dot(gram, columns, preferred_element_type=jnp.float32).astype(jnp.bfloat16)
        second = jnp.dot(
            gram, gather_directly(first, "tp", 0), preferred_element_type=jnp.float32
        ).astype(jnp.bfloat16)
        if step == 0:
            mixed = (
                first_coef * iterate.astype(jnp.float32) * root
                + second_coef * first.astype(jnp.float32) * root**3
                + third_coef * second.astype(jnp.float32) * root**5
            )
        else:
            mixed = (
                first_coef * iterate.astype(jnp.float32)
                + second_coef * first.astype(jnp.float32)
                + third_coef * second.astype(jnp.float32)
            )
        iterate = mixed.astype(jnp.bfloat16)
    update = (shape_gain * math.sqrt(max(R, C)) * iterate.astype(jnp.float32)).astype(jnp.bfloat16)
    return (update, new_momentum)


def solution(mesh):
    split = Mesh(
        mesh.devices.reshape(8, 4, 2, mesh.shape["tp"]), ("mats_0", "mats_1", "mats_2", "tp")
    )
    return jax.shard_map(
        per_device,
        mesh=split,
        in_specs=(P("tp", MATS), P("tp", MATS)),
        out_specs=(P("tp", MATS), P("tp", MATS)),
        check_vma=False,
    )
```

profile of v0, /device:TPU:1, one launch (start us, length us, event | category | flops | bytes accessed | tf_op | source)
XLA Modules:
  0.0 602.9 jit_solution(10310170198701383736)
XLA Ops:
  7.2 0.0 reduce-scatter.3.cloned.1.call-start
  7.2 2.3 fusion.11
  9.5 0.1 broadcast_in_dim.24
  9.6 24.7 %all_to_all.32 = bf16[4,768,256]{2,1,0:T(8,128)(2,1)S(1)} all-to-all(bf16[4,768,256]{2,1,0:T(8,128)(2,1)S(1)} %broadcast_in_dim.24), channel_id=1, replica_groups=mesh['mats_0'=8,'mats_1'=4,'mats_2'=2,'tp'=4] {'tp'}, dimensions={0} | all-to-all | bytes 3145728 | tf_op jit(solution)/shard_map/all_to_all | solution.py:31
  34.3 5.0 fusion.12
  39.3 0.0 reduce-scatter.3.cloned.1.call-update
  39.3 0.0 all-gather.7.cloned.1.call-start
  39.4 153.2 %reduce-scatter.3.cloned.1.call-done = f32[768,48]{0,1:T(8,128)} async-done(((f32[768,3072]{0,1:T(8,128)}), f32[768,48]{0,1:T(8,128)}) %reduce-scatter.3.cloned.1.call-update) | async-done | bytes 147472 | tf_op jit(solution)/shard_map/reduce_scatter | solution.py:74
  192.6 0.9 abs_reduce_fusion
  193.5 9.4 %all-gather = bf16[3072,48]{0,1:T(8,128)(2,1)S(1)} all-gather(bf16[768,48]{0,1:T(8,128)(2,1)S(1)} %get-tuple-element.3), channel_id=2, replica_groups=mesh['mats_0'=8,'mats_1'=4,'mats_2'=2,'tp'=4] {'mats_1'}, dimensions={0}, use_global_device_ids=true | all-gather | bytes 368640 | tf_op jit(solution)/shard_map/all_gather | solution.py:41
  202.9 0.7 copy.30
  203.7 0.0 all-gather.7.cloned.1.call-update
  203.7 0.0 all-gather.9.cloned.1.call-start
  203.8 43.3 %all-gather.7.cloned.1.call-done = bf16[32,768,48]{1,2,0:T(8,128)(2,1)} async-done(((bf16[4,768,48]{1,2,0:T(8,128)(2,1)}), bf16[32,768,48]{1,2,0:T(8,128)(2,1)}) %all-gather.7.cloned.1.call-update) | async-done | bytes 2359312 | tf_op jit(solution)/shard_map/all_gather | solution.py:41
  247.1 0.0 all-gather.9.cloned.1.call-update
  247.1 0.1 broadcast_in_dim.25
  247.2 23.6 %all_to_all.33 = f32[64,1,768]{2,1,0:T(1,128)S(1)} all-to-all(f32[64,1,768]{2,1,0:T(1,128)S(1)} %broadcast_in_dim.25), channel_id=1, replica_groups=mesh['mats_0'=8,'mats_1'=4,'mats_2'=2,'tp'=4] {'mats_0','mats_1','mats_2'}, dimensions={0} | all-to-all | bytes 393216 | tf_op jit(solution)/shard_map/all_to_all | solution.py:31
  270.8 0.1 reduce_sum.19
  270.9 0.6 reduce_max.18
  271.5 1.1 broadcast_in_dim.26
  272.6 4.0 all-to-all-start.2
  276.6 0.0 all-gather.9.cloned.1.call-done
  276.6 2.9 copy.19
  279.5 0.0 copy-start
  279.5 2.1 copy-done
  281.7 1.4 convolution_convert_fusion.3
  283.1 0.0 all-to-all-done.2
  283.1 1.3 broadcast_in_dim.28
  284.4 4.2 all-to-all-start.3
  288.6 0.0 reduce-scatter.5.cloned.1.call-start
  288.6 0.6 reduce_max.19
  289.9 18.3 %all-to-all-done.3 = bf16[4,768,256]{2,1,0:T(8,128)(2,1)S(1)} async-done(((bf16[4,768,256]{2,1,0:T(8,128)(2,1)}), bf16[4,768,256]{2,1,0:T(8,128)(2,1)S(1)}, u32[]{:S(2)}, u32[]{:S(2)}) %all-to-all-start.3) | async-done | bytes 1572896 | tf_op jit(solution)/shard_map/all_to_all | solution.py:31
  308.2 3.8 fusion.9
  312.0 0.1 broadcast_in_dim.29
  312.1 20.9 %all_to_all.34 = bf16[4,768,256]{2,1,0:T(8,128)(2,1)S(1)} all-to-all(bf16[4,768,256]{2,1,0:T(8,128)(2,1)S(1)} %broadcast_in_dim.29), channel_id=1, replica_groups=mesh['mats_0'=8,'mats_1'=4,'mats_2'=2,'tp'=4] {'tp'}, dimensions={0} | all-to-all | bytes 3145728 | tf_op jit(solution)/shard_map/all_to_all | solution.py:31
  332.9 5.0 fusion.13
  338.0 0.0 reduce-scatter.5.cloned.1.call-update
  338.0 0.0 all-gather.11.cloned.1.call-start
  338.1 148.1 %reduce-scatter.5.cloned.1.call-done = f32[768,48]{0,1:T(8,128)} async-done(((f32[768,3072]{0,1:T(8,128)}), f32[768,48]{0,1:T(8,128)}) %reduce-scatter.5.cloned.1.call-update) | async-done | bytes 147472 | tf_op jit(solution)/shard_map/reduce_scatter | solution.py:74
  486.1 0.9 convert_element_type.69
  487.1 9.4 %all-gather.1 = bf16[3072,48]{0,1:T(8,128)(2,1)S(1)} all-gather(bf16[768,48]{0,1:T(8,128)(2,1)S(1)} %convert_element_type.69), channel_id=3, replica_groups=mesh['mats_0'=8,'mats_1'=4,'mats_2'=2,'tp'=4] {'mats_1'}, dimensions={0}, use_global_device_ids=true | all-gather | bytes 368640 | tf_op jit(solution)/shard_map/all_gather | solution.py:41
  496.5 0.7 copy.29
  497.2 0.0 all-gather.11.cloned.1.call-update
  497.3 0.0 all-gather.13.cloned.1.call-start
  497.3 43.7 %all-gather.11.cloned.1.call-done = bf16[32,768,48]{1,2,0:T(8,128)(2,1)} async-done(((bf16[4,768,48]{1,2,0:T(8,128)(2,1)}), bf16[32,768,48]{1,2,0:T(8,128)(2,1)}) %all-gather.11.cloned.1.call-update) | async-done | bytes 2359312 | tf_op jit(solution)/shard_map/all_gather | solution.py:41
  541.0 0.0 all-gather.13.cloned.1.call-update
  541.0 24.6 %all-gather.13.cloned.1.call-done = bf16[64,768,48]{1,2,0:T(8,128)(2,1)} async-done(((bf16[32,768,48]{1,2,0:T(8,128)(2,1)}), bf16[64,768,48]{1,2,0:T(8,128)(2,1)}) %all-gather.13.cloned.1.call-update) | async-done | bytes 4718608 | tf_op jit(solution)/shard_map/all_gather | solution.py:41
  565.6 2.9 copy.21
  568.5 1.4 convolution_convert_fusion.1
  569.9 0.1 broadcast_in_dim.31
  570.0 23.9 %all_to_all.35 = bf16[4,768,256]{2,1,0:T(8,128)(2,1)S(1)} all-to-all(bf16[4,768,256]{2,1,0:T(8,128)(2,1)S(1)} %broadcast_in_dim.31), channel_id=1, replica_groups=mesh['mats_0'=8,'mats_1'=4,'mats_2'=2,'tp'=4] {'tp'}, dimensions={0} | all-to-all | bytes 3145728 | tf_op jit(solution)/shard_map/all_to_all | solution.py:31
  593.9 2.2 fusion.10
Async XLA Ops:
  7.2 185.4 %reduce-scatter.3.cloned.1.call-start = ((), (), s32[]{:S(2)}) async-start(), calls=%async_computation.8 | async-start | bytes 9584640 | tf_op jit(solution)/shard_map/reduce_scatter | solution.py:74
  39.3 207.7 %all-gather.7.cloned.1.call-start = ((), (), s32[]{:S(2)}) async-start(), calls=%async_computation.9 | async-start | bytes 2654208 | tf_op jit(solution)/shard_map/all_gather | solution.py:41
  203.7 72.9 %all-gather.9.cloned.1.call-start = ((), (), s32[]{:S(2)}) async-start(), calls=%async_computation.10 | async-start | bytes 7077888 | tf_op jit(solution)/shard_map/all_gather | solution.py:41
  272.6 10.5 %all-to-all-start.2 = ((f32[4,1,1]{2,1,0:T(1,128)}), f32[4,1,1]{2,1,0:T(1,128)S(1)}, u32[]{:S(2)}, u32[]{:S(2)}) async-start(f32[4,1,1]{2,1,0:T(1,128)} %broadcast_in_dim.26), calls=%async_computation.3 | async-start | bytes 4096 | tf_op jit(solution)/shard_map/all_to_all | solution.py:31
  279.5 2.1 copy-start
  284.4 23.8 %all-to-all-start.3 = ((bf16[4,768,256]{2,1,0:T(8,128)(2,1)}), bf16[4,768,256]{2,1,0:T(8,128)(2,1)S(1)}, u32[]{:S(2)}, u32[]{:S(2)}) async-start(bf16[4,768,256]{2,1,0:T(8,128)(2,1)} %broadcast_in_dim.28), calls=%async_computation.4 | async-start | bytes 3145728 | tf_op jit(solution)/shard_map/all_to_all | solution.py:31
  288.6 197.5 %reduce-scatter.5.cloned.1.call-start = ((), (), s32[]{:S(2)}) async-start(), calls=%async_computation.11 | async-start | bytes 9584640 | tf_op jit(solution)/shard_map/reduce_scatter | solution.py:74
  338.0 203.0 %all-gather.11.cloned.1.call-start = ((), (), s32[]{:S(2)}) async-start(), calls=%async_computation.12 | async-start | bytes 2654208 | tf_op jit(solution)/shard_map/all_gather | solution.py:41
  497.3 68.3 %all-gather.13.cloned.1.call-start = ((), (), s32[]{:S(2)}) async-start(), calls=%async_computation.13 | async-start | bytes 7077888 | tf_op jit(solution)/shard_map/all_gather | solution.py:41
Sparse Core Ops, SparseCore 0:
  39.4 153.0 reduce-scatter.2
  203.8 43.1 all-gather.6
  248.9 22.8 all-gather.8
  338.1 147.9 reduce-scatter.4
  497.4 43.5 all-gather.10
  542.6 22.8 all-gather.12
where the time goes:
time: 603 us
  waiting for transfers between devices  431 us (71%)
  blocking collectives  112 us (19%)
  matrix products  18.9 us (3%)
  between operations  14.9 us (2%)
  local copies, waits for them, and re-layouts  12.2 us (2%)
  starting transfers between devices  8.45 us (1%)
    reduce_scatter x2, waiting for transfers between devices, per_device(): lax.psum_scatter(partial_gram, MATS, scatter_dimension=1, tiled=True)  301 us
    all_gather x4, waiting for transfers between devices, gather_in_order(): tiles = lax.all_gather(tiles, axes[k], axis=0, tiled=True)  112 us
    all_to_all x4, blocking collectives, sent_to_all(): return lax.all_to_all(copies, axis, split_axis=0, concat_axis=0, tiled=True)  93 us
    all_gather x2, blocking collectives, gather_in_order(): tiles = lax.all_gather(tiles, axes[k], axis=0, tiled=True)  18.9 us
    all_to_all x2, waiting for transfers between devices, sent_to_all(): return lax.all_to_all(copies, axis, split_axis=0, concat_axis=0, tiled=True)  18.3 us
  transfers between devices with their start and end apart: 8, of which 6 were waited for; matrix products, arithmetic and copies ran while one was open for 1% of the time, Pallas kernels for 0%

commit v1 on v0

v1 whole, which is shorter than its diff:
```python
import math

import jax
import jax.numpy as jnp
from jax import lax
from jax.experimental import pallas as pl
from jax.experimental.pallas import tpu as pltpu
from jax.sharding import Mesh
from jax.sharding import PartitionSpec as P

R = 3072
C = 16384
AX = {"z": "mats_0", "x": "mats_1", "c": "mats_2", "y": "tp"}
SIZES = {"z": 8, "x": 4, "c": 2, "y": 4}

momentum_beta = 0.95
first_coef = 3.4445
second_coef = -4.775
third_coef = 2.0315
shape_gain = 0.2
epsilon = 1e-06

BF = jnp.bfloat16
F32 = jnp.float32
MESH = pl.DeviceIdType.MESH


def around(s, d, n):
    d = d % n
    return s if d == 0 else lax.rem(s + d, n)


class Comm:
    def __init__(self, send_sems, recv_sems):
        self.send_sems, self.recv_sems = send_sems, recv_sems
        self.next_send = self.next_recv = self.most_send = self.most_recv = 0
        self.open = []

    def recv_index(self):
        self.next_recv += 1
        self.most_recv = max(self.most_recv, self.next_recv)
        return self.next_recv - 1

    def start(self, src, dst, axis, to, index=None):
        if index is None:
            index = self.recv_index()
        copy = pltpu.make_async_remote_copy(
            src_ref=src,
            dst_ref=dst,
            send_sem=self.send_sems.at[self.next_send],
            recv_sem=self.recv_sems.at[index],
            device_id={AX[axis]: to},
            device_id_type=MESH,
        )
        self.next_send += 1
        self.most_send = max(self.most_send, self.next_send)
        copy.start()
        self.open.append(copy)
        return index

    def wait(self, dst, index, axis, peer):
        pltpu.make_async_remote_copy(
            src_ref=dst,
            dst_ref=dst,
            send_sem=self.send_sems.at[0],
            recv_sem=self.recv_sems.at[index],
            device_id={AX[axis]: peer},
            device_id_type=MESH,
        ).wait_recv()

    def drain(self):
        for copy in self.open:
            copy.wait_send()
        self.open = []
        self.next_send = 0


def tree(comm, me, n, a1, a2, slot, arrived):
    n1, n2 = n[a1], (n[a2] if a2 else 1)
    s1, s2 = me[a1], (me[a2] if a2 else 0)
    held = {}

    def ref(d1, d2, h):
        return slot(around(s1, d1, n1), around(s2, d2, n2), h)

    def send(level, d1, d2, hop, way):
        axis, size, s = (a1, n1, s1) if level == 1 else (a2, n2, s2)
        half = None if hop < size // 2 else (0 if way > 0 else 1)
        piece = ref(d1, d2, half)
        index = comm.start(piece, piece, axis, around(s, way, size))
        key = (1, d1 - way, d2, hop, way) if level == 1 else (2, d1, d2 - way, hop, way)
        held[key] = (index, half)

    def take(level, d1, d2, hop, way):
        index, half = held.pop((level, d1, d2, hop, way))
        axis, size, s = (a1, n1, s1) if level == 1 else (a2, n2, s2)
        comm.wait(ref(d1, d2, half), index, axis, around(s, way, size))

    def spread(d1):
        if n2 > 1:
            for way in (1, -1):
                send(2, d1, 0, 1, way)

    if n1 > 1:
        for way in (1, -1):
            send(1, 0, 0, 1, way)
    spread(0)
    arrived(0, 0)
    yield
    last1, last2 = n1 // 2, n2 // 2
    for hop in range(1, last1 + last2 + 1):
        if n1 > 1 and hop <= last1:
            for way in (1, -1):
                d1 = -hop * way
                take(1, d1, 0, hop, way)
                if hop < last1:
                    send(1, d1, 0, hop + 1, way)
                    spread(d1)
                    arrived(d1, 0)
            if hop == last1:
                spread(last1)
                arrived(last1, 0)
        for t1 in range(last1 + 1):
            t2 = hop - t1
            if n2 == 1 or not 1 <= t2 <= last2:
                continue
            for d1 in [0] if t1 == 0 else [last1] if t1 == last1 else [-t1, t1]:
                for way in (1, -1):
                    d2 = -t2 * way
                    take(2, d1, d2, t2, way)
                    if t2 < last2:
                        send(2, d1, d2, t2 + 1, way)
                        arrived(d1, d2)
                if t2 == last2:
                    arrived(d1, last2)
        yield


def together(*walks):
    walks = list(walks)
    while walks:
        for walk in list(walks):
            try:
                next(walk)
            except StopIteration:
                walks.remove(walk)


def add_into(target, source):
    def step(i, carry):
        target[i] = (target[i].astype(F32) + source[i].astype(F32)).astype(BF)
        return carry

    if len(target.shape) > 2:
        lax.fori_loop(0, target.shape[0], step, 0)
    else:
        target[...] = (target[...].astype(F32) + source[...].astype(F32)).astype(BF)


def ring_sum(comm, me, n, axis, piece, landing):
    size, s = n[axis], me[axis]
    if size == 1:
        return
    last = size // 2
    index = {}
    for hop in range(1, last + 1):
        for way in (1, -1):
            first = 0 if way > 0 else 1
            d = around(s, way * (last - hop + 1), size)
            to, source = around(s, way, size), around(s, -way, size)
            half = first if hop == 1 else None
            if hop > 1:
                came = first if hop == 2 else None
                comm.wait(landing(way, hop - 1, came), index[way, hop - 1], axis, source)
                add_into(piece(d, came), landing(way, hop - 1, came))
            index[way, hop] = comm.start(piece(d, half), landing(way, hop, half), axis, to)
    for way in (1, -1):
        half = None if last > 1 else (0 if way > 0 else 1)
        comm.wait(landing(way, last, half), index[way, last], axis, around(s, -way, size))
    comm.drain()


def kernel(
    n, gain, x_ref, o_ref, xc, part, z1, x1, z2, x2, gram, cube, rpg, cpg, rp2, cp2, rpp, cpp, rph, cps, rpn, cpw,
    qi, swap, edge, peaks, send_sems, recv_sems, local_sem,
):
    nz, nx, nc, ny = n["z"], n["x"], n["c"], n["y"]
    me = {a: (lax.axis_index(AX[a]) if n[a] > 1 else 0) for a in "zxcy"}
    z, x, c, y = me["z"], me["x"], me["c"], me["y"]
    rows_block, columns = x_ref.shape
    rows_half = rows_block // nc
    ph, pw = gram.shape
    half_rows = ph // 2
    mine = (y * nc + c) * nx + x
    comm = Comm(send_sems, recv_sems)

    barrier = pltpu.get_barrier_semaphore()
    peers = [(a, d) for a in "zxcy" for d in range(1, n[a]) if a != "z" or d in (1, n[a] - 1)]
    for a, d in peers:
        pl.semaphore_signal(barrier, inc=1, device_id={AX[a]: around(me[a], d, n[a])}, device_id_type=MESH)
    pl.semaphore_wait(barrier, len(peers))

    parts = 2
    share = rows_block // parts

    def x_slot(i, q, h):
        if h is None:
            return xc.at[c, i, pl.ds(q * share, share)]
        return xc.at[c, i, pl.ds(q * share + h * (share // 2), share // 2)]

    own = pltpu.make_async_copy(x_ref, xc.at[c, y], local_sem)
    own.start()
    own.wait()
    to_partner = {}

    def x_arrived(q):
        def done(d, _):
            if nc > 1:
                ref = x_slot(around(y, d, ny), q, None)
                to_partner[q, d % ny] = comm.start(ref, ref, "c", 1 - c)

        return done

    together(*(tree(comm, me, n, "y", None, lambda i, _, h, q=q: x_slot(i, q, h), x_arrived(q)) for q in range(parts)))
    for (q, d), index in to_partner.items():
        comm.wait(xc.at[1 - c, around(y, d, ny), pl.ds(q * share, share)], index, "c", 1 - c)
    comm.drain()

    per_block = rows_block // pw

    def gram_piece(d, carry):
        total = jnp.zeros((rows_half, pw), F32)
        for h in range(nc):
            left = xc[h, y, pl.ds(pl.multiple_of(c * rows_half, rows_half), rows_half)]
            right = xc[h, d // per_block, pl.ds(pl.multiple_of(d % per_block * pw, pw), pw)]
            total += lax.dot_general(left, right, (((1,), (1,)), ((), ())), preferred_element_type=F32)
        part[d] = total.astype(BF).reshape(nx, ph, pw)
        return carry

    lax.fori_loop(0, nz, gram_piece, 0)

    def two_halves(ref, h, length):
        return ref if h is None else ref.at[pl.ds(h * length, length)]

    def finish(extra):
        total = part[z, x].astype(F32)
        for ref in extra:
            total += ref[...].astype(F32)
        gram[...] = total

    sums_base = comm.next_recv
    for core in range(nc):

        @pl.when(c == core)
        def _():
            comm.next_recv = sums_base
            if core == 0:
                ring_sum(
                    comm, me, n, "z",
                    lambda d, h: part.at[d] if h is None else part.at[d, pl.ds(h * (nx // 2), nx // 2)],
                    lambda way, hop, h: (
                        z1.at[int(way > 0), hop - 1] if h is None else z1.at[int(way > 0), hop - 1, pl.ds(h * (nx // 2), nx // 2)]
                    ),
                )
                if nz > 1:
                    for way in (0, 1):
                        add_into(part.at[z], z1.at[way, nz // 2 - 1])
                ring_sum(
                    comm, me, n, "x",
                    lambda d, h: two_halves(part.at[z, d], h, half_rows),
                    lambda way, hop, h: two_halves(x2.at[int(way > 0), hop - 1], h, half_rows),
                )
                finish([x2.at[way, nx // 2 - 1] for way in (0, 1)] if nx > 1 else [])
            else:
                ring_sum(
                    comm, me, n, "x",
                    lambda d, h: part.at[:, d] if h is None else part.at[pl.ds(h * (nz // 2), nz // 2), d],
                    lambda way, hop, h: (
                        x1.at[int(way > 0), hop - 1] if h is None else x1.at[int(way > 0), hop - 1, pl.ds(h * (nz // 2), nz // 2)]
                    ),
                )
                if nx > 1:
                    for way in (0, 1):
                        add_into(part.at[:, x], x1.at[way, nx // 2 - 1])
                ring_sum(
                    comm, me, n, "z",
                    lambda d, h: two_halves(part.at[d, x], h, half_rows),
                    lambda way, hop, h: two_halves(z2.at[int(way > 0), hop - 1], h, half_rows),
                )
                finish([z2.at[way, nz // 2 - 1] for way in (0, 1)] if nz > 1 else [])


    comm.next_recv = comm.most_recv

    def panels(rp, cp, base, peak=False):
        pieces = ny * nx
        for core in range(nc):

            @pl.when(c == core)
            def _():
                comm.next_recv = base + pieces + 1
                a1, a2 = ("y", "x") if core == 0 else ("x", "y")
                if n[a1] == 1:
                    a1, a2 = a2, a1

                def spot(i1, i2):
                    iy, ix = (i1, i2) if a1 == "y" else (i2, i1)
                    return (iy * nc + core) * nx + ix

                def slot(i1, i2, h):
                    return two_halves(cp.at[spot(i1, i2)], h, half_rows)

                def arrived(d1, d2):
                    if nc > 1:
                        dy, dx = (d1, d2) if a1 == "y" else (d2, d1)
                        ref = slot(around(me[a1], d1, n[a1]), around(me[a2], d2, n[a2]), None)
                        comm.start(ref, ref, "c", 1 - c, base + dy % ny * nx + dx % nx)

                def largest():
                    yield
                    kept = edge[0]
                    for axis, at in (("y", 1), ("x", 1 + ny), ("c", 1 + ny + nx)):
                        if n[axis] == 1:
                            continue
                        edge[at] = kept
                        index = {}
                        for d in range(1, n[axis]):
                            index[d] = comm.start(
                                edge.at[at], edge.at[at + d], axis, around(me[axis], d, n[axis]),
                                base + pieces if axis == "c" else None,
                            )
                        yield
                        for d in range(1, n[axis]):
                            comm.wait(edge.at[at + d], index[d], axis, around(me[axis], -d, n[axis]))
                            kept = jnp.maximum(kept, edge[at + d])
                    peaks[...] = kept

                walks = [
                    tree(comm, me, n, "z", None, lambda i, _, h: two_halves(rp.at[i], h, half_rows), lambda d, _: None),
                    tree(comm, me, n, a1, a2, slot, arrived),
                ]
                together(*walks, *([largest()] if peak else []))
                if nc > 1:
                    for dy in range(ny):
                        for dx in range(nx):
                            ref = cp.at[(around(y, dy, ny) * nc + 1 - core) * nx + around(x, dx, nx)]
                            comm.wait(ref, base + dy * nx + dx, "c", 1 - c)
                comm.drain()

        comm.next_recv = max(comm.next_recv, comm.most_recv)

    def put(value, rp, cp):
        value = value.astype(BF)
        if rp is not None:
            rp[z] = value
        if cp is not None:
            cp[mine] = value

    per_chunk = cpg.shape[0] // nz

    def times(rps, cp):
        def step(k, totals):
            right = cp[pl.ds(k * per_chunk, per_chunk)].reshape(per_chunk * ph, pw)
            return tuple(t + jnp.dot(rp[k], right, preferred_element_type=F32) for t, rp in zip(totals, rps))

        return lax.fori_loop(0, nz, step, tuple(jnp.zeros((ph, pw), F32) for _ in rps))

    def with_identity(value, row, column, scale):
        rows = lax.broadcasted_iota(jnp.int32, value.shape, 0) + row
        across = lax.broadcasted_iota(jnp.int32, value.shape, 1) + column
        return value + jnp.where(rows == across, scale, 0.0)

    put(gram[...], rpg, cpg)
    panels(rpg, cpg, comm.next_recv)

    def sizes(k, total):
        return total + jnp.abs(rpg[k].astype(F32))

    row_sums = jnp.sum(lax.fori_loop(0, nz, sizes, jnp.zeros((ph, pw), F32)), axis=1, keepdims=True)
    edge[0] = jnp.broadcast_to(jnp.max(row_sums, axis=0, keepdims=True), edge.shape[1:])
    (square,) = times([rpg], cpg)
    put(square, rp2, cp2)
    panels(rp2, cp2, comm.next_recv, peak=True)

    bound = jnp.max(jnp.max(peaks[...], axis=1, keepdims=True), axis=0, keepdims=True) + epsilon
    inverse = 1.0 / bound
    root = lax.rsqrt(bound)

    def mix(once, twice, row, column):
        value = second_coef * (once.astype(F32) * inverse) + third_coef * (twice.astype(F32) * inverse * inverse)
        return with_identity(value, row, column, first_coef)

    def mix_rows(k, carry):
        rpp[k] = mix(rpg[k], rp2[k], mine * ph, k * pw).astype(BF)
        return carry

    def mix_columns(k, carry):
        cpp[k] = mix(cpg[k], cp2[k], k * ph, z * pw).astype(BF)
        return carry

    lax.fori_loop(0, nz, mix_rows, 0)
    lax.fori_loop(0, cpp.shape[0], mix_columns, 0)
    cube[...] = mix(gram[...], square, mine * ph, z * pw)

    (once,) = times([rpg], cpp)
    (twice,) = times([rpp], cpp)
    put(once * inverse, rph, None)
    put(twice, None, cps)
    panels(rph, cps, comm.next_recv)
    (next_gram,) = times([rph], cpp)
    (next_first,) = times([rph], cps)
    put(next_gram, rpn, None)
    put(next_first, None, cpw)
    panels(rpn, cpw, comm.next_recv)
    (next_second,) = times([rpn], cpw)
    whole = (gain * root) * (first_coef * cube[...] + second_coef * next_first + third_coef * next_second)
    qi[z, x] = whole.astype(BF)

    sums_base = comm.next_recv
    for core in range(nc):

        @pl.when(c == core)
        def _():
            comm.next_recv = sums_base
            a1, a2 = ("z", "x") if core == 0 else ("x", "z")
            if n[a1] == 1:
                a1, a2 = a2, a1

            def slot(i1, i2, h):
                iz, ix = (i1, i2) if a1 == "z" else (i2, i1)
                return two_halves(qi.at[iz, ix], h, half_rows)

            together(tree(comm, me, n, a1, a2, slot, lambda d1, d2: None))
            comm.drain()

    comm.next_recv = comm.most_recv

    def product(side):
        def step(k, total):
            left = qi[k].reshape(rows_half, pw)
            right = xc[side, k // per_block, pl.ds(pl.multiple_of(k % per_block * pw, pw), pw)]
            return total + jnp.dot(left, right, preferred_element_type=F32)

        return lax.fori_loop(0, nz, step, jnp.zeros((rows_half, columns), F32)).astype(BF)

    if nc > 1:
        swap[0] = product(1 - c)
        index = comm.start(swap.at[0], swap.at[1], "c", 1 - c)
    o_ref[pl.ds(pl.multiple_of(c * rows_half, rows_half), rows_half)] = product(c)
    if nc > 1:
        comm.wait(swap.at[1], index, "c", 1 - c)
        o_ref[pl.ds(pl.multiple_of((1 - c) * rows_half, rows_half), rows_half)] = swap[1]
        comm.drain()


def update_call(n, gain, x):
    nz, nx, nc, ny = n["z"], n["x"], n["c"], n["y"]
    rows_block, columns = x.shape
    rows = rows_block * ny
    ph, pw = rows // (ny * nc * nx), rows // nz
    pieces = ny * nc * nx
    row_panel = pltpu.VMEM((nz, ph, pw), BF)
    column_panel = pltpu.VMEM((pieces, ph, pw), BF)
    hops_z, hops_x = max(nz // 2, 1), max(nx // 2, 1)
    tiles = 2 + ny + nx + nc
    return pl.pallas_call(
        lambda *refs: kernel(n, gain, *refs),
        out_shape=jax.ShapeDtypeStruct(x.shape, BF),
        in_specs=[pl.BlockSpec(memory_space=pltpu.VMEM)],
        out_specs=pl.BlockSpec(memory_space=pltpu.VMEM),
        scratch_shapes=[
            pltpu.VMEM((nc, ny, rows_block, columns), BF),
            pltpu.VMEM((nz, nx, ph, pw), BF),
            pltpu.VMEM((2, hops_z, nx, ph, pw), BF),
            pltpu.VMEM((2, hops_x, nz, ph, pw), BF),
            pltpu.VMEM((2, hops_z, ph, pw), BF),
            pltpu.VMEM((2, hops_x, ph, pw), BF),
            pltpu.VMEM((ph, pw), F32),
            pltpu.VMEM((ph, pw), F32),
            row_panel, column_panel, row_panel, column_panel, row_panel, column_panel,
            row_panel, column_panel, row_panel, column_panel,
            pltpu.VMEM((nz, nx, ph, pw), BF),
            pltpu.VMEM((2, rows_block // nc, columns), BF),
            pltpu.VMEM((tiles, 8, 128), F32),
            pltpu.VMEM((8, 128), F32),
            pltpu.SemaphoreType.DMA((80,)),
            pltpu.SemaphoreType.DMA((300,)),
            pltpu.SemaphoreType.DMA,
        ],
        compiler_params=pltpu.CompilerParams(
            collective_id=0, has_side_effects=True, vmem_limit_bytes=48 * 1024 * 1024
        ),
    )(x)


def per_device(grad, momentum):
    new_momentum = momentum_beta * momentum + grad.astype(F32)
    iterate = (grad.astype(F32) + momentum_beta * new_momentum).astype(BF)
    update = update_call(SIZES, shape_gain * math.sqrt(max(R, C)), iterate)
    return (update, new_momentum)


def solution(mesh):
    devices = mesh.devices.reshape(SIZES["z"], SIZES["x"], SIZES["c"], SIZES["y"])
    split = Mesh(devices, (AX["z"], AX["x"], AX["c"], AX["y"]))
    mats = (AX["z"], AX["x"], AX["c"])
    return jax.shard_map(
        per_device,
        mesh=split,
        in_specs=(P(AX["y"], mats), P(AX["y"], mats)),
        out_specs=(P(AX["y"], mats), P(AX["y"], mats)),
        check_vma=False,
    )
```

time: 603 us -> 182 us (0.30)
  waiting for transfers between devices: 431 us -> 0 us
  Pallas kernels: 0 us -> 178 us
  blocking collectives: 112 us -> 0 us
  matrix products: 18.9 us -> 0 us
  between operations: 14.9 us -> 0.64 us
  local copies, waits for them, and re-layouts: 12.2 us -> 0.75 us
  starting transfers between devices: 8.45 us -> 0 us
    reduce_scatter x2 -> x0, waiting for transfers between devices: 301 us -> none  [per_device(): lax.psum_scatter(partial_gram, MATS, scatter_dimension=1, tiled=True)]
    pallas_call x0 -> x1, Pallas kernels: none -> 178 us  [update_call(): pl.pallas_call(lambda *refs: kernel(n, gain, *refs), out_shape=jax.ShapeD...]
    all_gather x4 -> x0, waiting for transfers between devices: 112 us -> none  [gather_in_order(): tiles = lax.all_gather(tiles, axes[k], axis=0, tiled=True)]
    all_to_all x4 -> x0, blocking collectives: 93 us -> none  [sent_to_all(): return lax.all_to_all(copies, axis, split_axis=0, concat_axis=0, tiled=True)]
    dot_general x6 -> x0, matrix products: 18.9 us -> none  [the longest x2 10.1 us: row_dot(): lax.dot_general(left, right, (((1,), (1,)), ((), ())), preferred_element_...]
    all_gather x2 -> x0, blocking collectives: 18.9 us -> none  [gather_in_order(): tiles = lax.all_gather(tiles, axes[k], axis=0, tiled=True)]
    all_to_all x2 -> x0, waiting for transfers between devices: 18.3 us -> none  [sent_to_all(): return lax.all_to_all(copies, axis, split_axis=0, concat_axis=0, tiled=True)]
    all_to_all x2 -> x0, starting transfers between devices: 8.24 us -> none  [sent_to_all(): return lax.all_to_all(copies, axis, split_axis=0, concat_axis=0, tiled=True)]
  transfers between devices with their start and end apart: 8 -> 0, of which waited for: 6 -> 0; matrix products, arithmetic and copies ran while one was open for 1% -> 0% of each run, Pallas kernels for 0% -> 0%
where the time goes in v1:
time: 182 us
  Pallas kernels  178 us (98%)
  other arithmetic  2.28 us (1%)
    pallas_call x1, Pallas kernels, update_call(): pl.pallas_call(lambda *refs: kernel(n, gain, *refs), out_shape=jax.ShapeD...  178 us

profile of v1, /device:TPU:1, one launch (start us, length us, event | category | flops | bytes accessed | tf_op | source)
XLA Modules:
  0.0 181.8 jit_solution(15077154121297505010)
XLA Ops:
  0.6 2.3 %fusion = (bf16[768,256]{1,0:T(8,128)(2,1)S(1)}, f32[768,256]{1,0:T(8,128)}) fusion(bf16[768,256]{1,0:T(8,128)(2,1)} %param.2, f32[768,256]{1,0:T(8,128)} %param.3), kind=kLoop, calls=%fused_computation.2 | loop fusion | flops 1179648 | bytes 2359296 | tf_op jit(solution)/shard_map/convert_element_type | solution.py:498
  2.9 178.1 %shard_map.41 = bf16[768,256]{1,0:T(8,128)(2,1)S(1)} custom-call(bf16[768,256]{1,0:T(8,128)(2,1)S(1)} %get-tuple-element.2.refs_0_), custom_call_target="tpu_custom_call" | custom-call | tf_op jit(solution)/shard_map/pallas_call | solution.py:466
  181.0 0.7 copy.5

commit v2 on v1

v2 whole, which is shorter than its diff:
```python
import math

import jax
import jax.numpy as jnp
from jax import lax
from jax.experimental import pallas as pl
from jax.experimental.pallas import tpu as pltpu
from jax.sharding import Mesh
from jax.sharding import PartitionSpec as P

R = 3072
C = 16384
AX = {"z": "mats_0", "x": "mats_1", "c": "mats_2", "y": "tp"}
SIZES = {"z": 8, "x": 4, "c": 2, "y": 4}

momentum_beta = 0.95
first_coef = 3.4445
second_coef = -4.775
third_coef = 2.0315
shape_gain = 0.2
epsilon = 1e-06

BF = jnp.bfloat16
F32 = jnp.float32
MESH = pl.DeviceIdType.MESH


def around(s, d, n):
    d = d % n
    return s if d == 0 else lax.rem(s + d, n)


class Comm:
    def __init__(self, send_sems, recv_sems):
        self.send_sems, self.recv_sems = send_sems, recv_sems
        self.next_send = self.next_recv = self.most_recv = 0
        self.open = []

    def recv_index(self):
        self.next_recv += 1
        self.most_recv = max(self.most_recv, self.next_recv)
        return self.next_recv - 1

    def send_index(self):
        self.next_send += 1
        return self.next_send - 1

    def start(self, src, dst, axis, to, index=None, send=None):
        if index is None:
            index = self.recv_index()
        kept = send is None
        if kept:
            send = self.send_index()
        copy = pltpu.make_async_remote_copy(
            src_ref=src,
            dst_ref=dst,
            send_sem=self.send_sems.at[send],
            recv_sem=self.recv_sems.at[index],
            device_id={AX[axis]: to},
            device_id_type=MESH,
        )
        copy.start()
        if kept:
            self.open.append(copy)
        return index

    def handle(self, ref, send, index, axis, peer):
        return pltpu.make_async_remote_copy(
            src_ref=ref,
            dst_ref=ref,
            send_sem=self.send_sems.at[send],
            recv_sem=self.recv_sems.at[index],
            device_id={AX[axis]: peer},
            device_id_type=MESH,
        )

    def wait(self, ref, index, axis, peer):
        self.handle(ref, 0, index, axis, peer).wait_recv()

    def wait_sent(self, ref, send, axis, peer):
        self.handle(ref, send, 0, axis, peer).wait_send()

    def drain(self):
        for copy in self.open:
            copy.wait_send()
        self.next_send -= len(self.open)
        self.open = []


def ring_relay(comm, me, n, axis, slot, arrived):
    size, s = n[axis], me[axis]
    at = lambda d: around(s, d, size)
    send = comm.send_index()
    near, far = comm.recv_index(), {1: comm.recv_index(), -1: comm.recv_index()}
    own = slot(s, None)
    for way in (1, -1):
        comm.start(own, own, axis, at(2 * way), far[way], send)
    for way in (1, -1):
        comm.start(own, own, axis, at(way), near, send)
    yield
    for way in (1, -1):
        piece = slot(at(-2 * way), None)
        comm.wait(piece, far[way], axis, at(-2 * way))
        comm.start(piece, piece, axis, at(way), near, send)
        half = slot(at(-2 * way), 0 if way > 0 else 1)
        comm.start(half, half, axis, at(2 * way), near, send)
    yield
    arrived(near, send)


def tree(comm, me, n, a1, a2, slot, arrived):
    n1, n2 = n[a1], (n[a2] if a2 else 1)
    s1, s2 = me[a1], (me[a2] if a2 else 0)
    held = {}

    def ref(d1, d2, h):
        return slot(around(s1, d1, n1), around(s2, d2, n2), h)

    def send(level, d1, d2, hop, way):
        axis, size, s = (a1, n1, s1) if level == 1 else (a2, n2, s2)
        half = None if hop < size // 2 else (0 if way > 0 else 1)
        piece = ref(d1, d2, half)
        index = comm.start(piece, piece, axis, around(s, way, size))
        key = (1, d1 - way, d2, hop, way) if level == 1 else (2, d1, d2 - way, hop, way)
        held[key] = (index, half)

    def take(level, d1, d2, hop, way):
        index, half = held.pop((level, d1, d2, hop, way))
        axis, size, s = (a1, n1, s1) if level == 1 else (a2, n2, s2)
        comm.wait(ref(d1, d2, half), index, axis, around(s, way, size))

    def spread(d1):
        if n2 > 1:
            for way in (1, -1):
                send(2, d1, 0, 1, way)

    if n1 > 1:
        for way in (1, -1):
            send(1, 0, 0, 1, way)
    spread(0)
    arrived(0, 0)
    yield
    last1, last2 = n1 // 2, n2 // 2
    for hop in range(1, last1 + last2 + 1):
        if n1 > 1 and hop <= last1:
            for way in (1, -1):
                d1 = -hop * way
                take(1, d1, 0, hop, way)
                if hop < last1:
                    send(1, d1, 0, hop + 1, way)
                    spread(d1)
                    arrived(d1, 0)
            if hop == last1:
                spread(last1)
                arrived(last1, 0)
        for t1 in range(last1 + 1):
            t2 = hop - t1
            if n2 == 1 or not 1 <= t2 <= last2:
                continue
            for d1 in [0] if t1 == 0 else [last1] if t1 == last1 else [-t1, t1]:
                for way in (1, -1):
                    d2 = -t2 * way
                    take(2, d1, d2, t2, way)
                    if t2 < last2:
                        send(2, d1, d2, t2 + 1, way)
                        arrived(d1, d2)
                if t2 == last2:
                    arrived(d1, last2)
        yield


def together(*walks):
    walks = list(walks)
    while walks:
        for walk in list(walks):
            try:
                next(walk)
            except StopIteration:
                walks.remove(walk)


def kernel(
    n, gain, x_ref, o_ref, xc, part, z1, x1, z2, x2, gram, cube, sums, rpg, cpg, rp2, cp2, rpp, cpp, rph, cps, rpn, cpw,
    qi, swap, edge, peaks, send_sems, recv_sems, local_sem,
):
    nz, nx, nc, ny = n["z"], n["x"], n["c"], n["y"]
    me = {a: (lax.axis_index(AX[a]) if n[a] > 1 else 0) for a in "zxcy"}
    z, x, c, y = me["z"], me["x"], me["c"], me["y"]
    rows_block, columns = x_ref.shape
    rows_half = rows_block // nc
    ph, pw = gram.shape
    half_rows = ph // 2
    mine = (y * nc + c) * nx + x
    comm = Comm(send_sems, recv_sems)

    barrier = pltpu.get_barrier_semaphore()
    peers = [(a, d) for a in "zxcy" for d in range(1, n[a])]
    for a, d in peers:
        pl.semaphore_signal(barrier, inc=1, device_id={AX[a]: around(me[a], d, n[a])}, device_id_type=MESH)
    pl.semaphore_wait(barrier, len(peers))

    parts = 2
    share = rows_block // parts

    def x_slot(i, q, h):
        if h is None:
            return xc.at[c, i, pl.ds(q * share, share)]
        return xc.at[c, i, pl.ds(q * share + h * (share // 2), share // 2)]

    own = pltpu.make_async_copy(x_ref, xc.at[c, y], local_sem)
    own.start()
    own.wait()
    to_partner = {}

    def x_arrived(q):
        def done(d, _):
            if nc > 1:
                ref = x_slot(around(y, d, ny), q, None)
                to_partner[q, d % ny] = comm.start(ref, ref, "c", 1 - c)

        return done

    together(*(tree(comm, me, n, "y", None, lambda i, _, h, q=q: x_slot(i, q, h), x_arrived(q)) for q in range(parts)))
    for (q, d), index in to_partner.items():
        comm.wait(xc.at[1 - c, around(y, d, ny), pl.ds(q * share, share)], index, "c", 1 - c)
    comm.drain()

    per_block = rows_block // pw
    top = pl.multiple_of(c * rows_half, rows_half)

    def right_rows(h, d):
        return xc[h, d // per_block, pl.ds(pl.multiple_of(d % per_block * pw, pw), pw)]

    def outer(left, right):
        return lax.dot_general(left, right, (((1,), (1,)), ((), ())), preferred_element_type=F32)

    def part_columns(d):
        total = sum(outer(xc[h, y, pl.ds(top, rows_half)], right_rows(h, d)) for h in range(nc))
        part[d] = total.astype(BF).reshape(nx, ph, pw)

    def part_rows(d):
        rows = pl.ds(pl.multiple_of(top + d * ph, ph), ph)

        def step(k, carry):
            part[k, d] = sum(outer(xc[h, y, rows], right_rows(h, k)) for h in range(nc)).astype(BF)
            return carry

        lax.fori_loop(0, nz, step, 0)

    def plus(piece, *more):
        total = piece[...].astype(F32)
        for other in more:
            total += other[...].astype(F32)
        return total

    def plane_sum(axis, piece, landing, chunks, prepare, across, final_landing):
        size, s = n[axis], me[axis]
        last = size // 2
        halves = {1: chunks[: len(chunks) // 2], -1: chunks[len(chunks) // 2 :]}
        index = {}
        send, final_send, final = comm.send_index(), comm.send_index(), comm.recv_index()

        def go(way, hop, e):
            index[way, hop, e] = comm.recv_index()
            d = around(s, way * (last - hop + 1), size)
            comm.start(piece(d, e), landing(way, hop, e), axis, around(s, way, size), index[way, hop, e], send)

        def come(way, hop, e):
            comm.wait(landing(way, hop, e), index[way, hop, e], axis, around(s, -way, size))
            return landing(way, hop, e)

        prepare(around(s, last, size))
        for a, b in zip(halves[1], halves[-1]):
            go(1, 1, a)
            go(-1, 1, b)
        for hop in range(2, last + 1):
            for way in (1, -1):
                prepare(around(s, way * (last - hop + 1), size))
                if hop == 2:
                    for e in halves[-way]:
                        go(way, hop, e)
            for k in range(len(chunks)):
                for way in (1, -1):
                    order = halves[way] if hop == 2 else halves[-way] + halves[way]
                    if k < len(order):
                        e = order[k]
                        ref = piece(around(s, way * (last - hop + 1), size), e)
                        ref[...] = plus(ref, come(way, hop - 1, e)).astype(BF)
                        go(way, hop, e)
        prepare(s)
        order = [e for pair in zip(halves[1], halves[-1]) for e in pair]
        for e in order:
            ref = piece(s, e)
            total = plus(ref, come(1, last, e), come(-1, last, e))
            if e == 0:
                gram[...] = total
            else:
                ref[...] = total.astype(BF)
                comm.start(ref, final_landing.at[e - 1], across, around(me[across], e, n[across]), final, final_send)
        comm.wait(final_landing, final, across, around(me[across], 1, n[across]))
        gram[...] = plus(gram, *(final_landing.at[k] for k in range(n[across] - 1)))
        comm.wait_sent(blocks((size - 1) * len(chunks)), send, axis, around(s, 1, size))
        comm.wait_sent(final_landing, final_send, across, around(me[across], 1, n[across]))

    def two_halves(ref, h, length):
        return ref if h is None else ref.at[pl.ds(h * length, length)]

    def blocks(count):
        across = next(k for k in range(nx, 0, -1) if count % k == 0 and count // k <= nz)
        return part.at[pl.ds(0, count // across), pl.ds(0, across)]

    base_recv, base_send = comm.next_recv, comm.next_send
    for core in range(nc):

        @pl.when(c == core)
        def _():
            comm.next_recv, comm.next_send = base_recv, base_send
            if core == 0:
                plane_sum(
                    "z", lambda d, e: part.at[d, around(x, e, nx)], lambda way, hop, e: z1.at[int(way > 0), hop - 1, e],
                    [2, 1, 3, 0], part_columns, "x", x2,
                )
            else:
                plane_sum(
                    "x", lambda d, e: part.at[around(z, e, nz), d], lambda way, hop, e: x1.at[int(way > 0), hop - 1, e],
                    [4, 5, 2, 7, 3, 6, 1, 0], part_rows, "z", z2,
                )

    comm.next_recv = comm.most_recv

    unsent = []

    def panels(rp, cp, half_done, peak=False):
        base_recv, base_send = comm.next_recv, comm.next_send
        for core in range(nc):

            @pl.when(c == core)
            def _():
                comm.next_recv, comm.next_send = base_recv, base_send
                over, peak_over = comm.recv_index(), comm.recv_index()
                send, send_over = comm.send_index(), comm.send_index()
                a1, a2 = ("y", "x") if core == 0 else ("x", "y")
                n1, n2 = n[a1], n[a2]
                at1, at2 = (lambda d: around(me[a1], d, n1)), (lambda d: around(me[a2], d, n2))

                def spot(d1, d2, h=None):
                    iy, ix = (at1(d1), at2(d2)) if a1 == "y" else (at2(d2), at1(d1))
                    return cp.at[iy, core, ix] if h is None else cp.at[iy, core, ix, pl.ds(h * half_rows, half_rows)]

                def group(d2):
                    return cp.at[:, core, at2(d2)] if a1 == "y" else cp.at[at2(d2), core]

                def to_partner(d2):
                    comm.start(group(d2), group(d2), "c", 1 - c, over, send_over)

                near1, far1, last = comm.recv_index(), comm.recv_index(), comm.recv_index()
                hop2 = {(way, k): comm.recv_index() for way in (1, -1) for k in range(3)}

                def spread(d1, k):
                    for way in (1, -1):
                        comm.start(spot(d1, 0), spot(d1, 0), a2, at2(way), hop2[way, k], send)
                    if d1 == 2:
                        comm.start(spot(d1, 0), spot(d1, 0), a2, at2(2), last, send)

                def pass_on(way, d1s):
                    for d1 in d1s:
                        half = spot(d1, -way, 0 if way > 0 else 1)
                        comm.start(half, half, a2, at2(way), last, send)

                def several(count):
                    return blocks(count)

                z_left = []
                z_walk = ring_relay(
                    comm, me, n, "z", lambda i, h: two_halves(rp.at[i], h, half_rows), lambda *left: z_left.append(left)
                )
                own = spot(0, 0)
                comm.start(own, own, a1, at1(2), far1, send)
                for way in (1, -1):
                    comm.start(own, own, a1, at1(way), near1, send)
                next(z_walk)
                spread(0, 0)
                peak_walk = largest(peak_over) if peak else iter(())
                next(peak_walk, None)

                comm.wait(several(2), near1, a1, at1(1))
                spread(-1, 1)
                spread(1, 1)
                for way in (1, -1):
                    comm.wait(own, hop2[way, 0], a2, at2(way))
                    pass_on(way, [0])
                comm.wait(own, far1, a1, at1(2))
                spread(2, 2)
                to_partner(0)
                next(z_walk)
                next(peak_walk, None)
                for way in (1, -1):
                    comm.wait(several(2), hop2[way, 1], a2, at2(way))
                    pass_on(way, [-1, 1])
                for way in (1, -1):
                    comm.wait(own, hop2[way, 2], a2, at2(way))
                    to_partner(-way)
                next(peak_walk, None)
                next(z_walk, None)
                comm.wait(several(4), last, a2, at2(1))
                to_partner(2)
                ((near, z_send),) = z_left
                comm.wait(rp.at[pl.ds(0, nz - 3)], near, "z", around(z, 1, nz))
                next(peak_walk, None)
                half_done()
                comm.wait(several(16), over, "c", 1 - c)
                if core == 0:
                    unsent.append((7, z_send, "z"))
                    unsent.append((15, send, "y"))
                    unsent.append((16, send_over, "c"))

        comm.next_recv = comm.most_recv

    def largest(over):
        kept = edge[0]
        sends = []
        for axis, at in (("y", 1), ("x", 1 + ny), ("c", 1 + ny + nx)):
            edge[at] = kept
            index, send = over if axis == "c" else comm.recv_index(), comm.send_index()
            for d in range(1, n[axis]):
                comm.start(edge.at[at], edge.at[at + d], axis, around(me[axis], d, n[axis]), index, send)
            yield
            comm.wait(edge.at[pl.ds(at + 1, n[axis] - 1)], index, axis, around(me[axis], 1, n[axis]))
            comm.wait_sent(edge.at[pl.ds(at + 1, n[axis] - 1)], send, axis, around(me[axis], 1, n[axis]))
            for d in range(1, n[axis]):
                kept = jnp.maximum(kept, edge[at + d])
        peaks[...] = kept

    def put(value, rp, cp):
        value = value.astype(BF)
        if rp is not None:
            rp[z] = value
        if cp is not None:
            cp[y, c, x] = value

    def times(rps, cp, core=None, totals=None):
        def step(k, totals):
            at = k if core is None else k * nc + core
            right = cp[at // nc, at % nc].reshape(nx * ph, pw)
            return tuple(t + jnp.dot(rp[at], right, preferred_element_type=F32) for t, rp in zip(totals, rps))

        if totals is None:
            totals = tuple(jnp.zeros((ph, pw), F32) for _ in rps)
        return lax.fori_loop(0, nz if core is None else nz // nc, step, totals)

    def exchange_and_times(rp, cp, pairs, peak=False):
        def half_done():
            at = 0
            for rps, right in pairs:
                for total in times(rps, right, c):
                    sums[at] = total
                    at += 1

        panels(rp, cp, half_done, peak)
        results, at = [], 0
        for rps, right in pairs:
            results += times(rps, right, 1 - c, tuple(sums[at + k] for k in range(len(rps))))
            at += len(rps)
        return results

    def with_identity(value, row, column, scale):
        rows = lax.broadcasted_iota(jnp.int32, value.shape, 0) + row
        across = lax.broadcasted_iota(jnp.int32, value.shape, 1) + column
        return value + jnp.where(rows == across, scale, 0.0)

    put(gram[...], rpg, cpg)
    (square,) = exchange_and_times(rpg, cpg, [([rpg], cpg)])

    def sizes(k, total):
        return total + jnp.abs(rpg[k].astype(F32))

    row_sums = jnp.sum(lax.fori_loop(0, nz, sizes, jnp.zeros((ph, pw), F32)), axis=1, keepdims=True)
    edge[0] = jnp.broadcast_to(jnp.max(row_sums, axis=0, keepdims=True), edge.shape[1:])
    put(square, rp2, cp2)
    panels(rp2, cp2, lambda: None, peak=True)

    bound = jnp.max(jnp.max(peaks[...], axis=1, keepdims=True), axis=0, keepdims=True) + epsilon
    inverse = 1.0 / bound
    root = lax.rsqrt(bound)

    def mix(once, twice, row, column):
        value = second_coef * (once.astype(F32) * inverse) + third_coef * (twice.astype(F32) * inverse * inverse)
        return with_identity(value, row, column, first_coef)

    def mix_rows(k, carry):
        rpp[k] = mix(rpg[k], rp2[k], mine * ph, k * pw).astype(BF)
        return carry

    def mix_columns(k, carry):
        at = (k // (nc * nx), k // nx % nc, k % nx)
        cpp[at] = mix(cpg[at], cp2[at], k * ph, z * pw).astype(BF)
        return carry

    lax.fori_loop(0, nz, mix_rows, 0)
    lax.fori_loop(0, ny * nc * nx, mix_columns, 0)
    cube[...] = mix(gram[...], square, mine * ph, z * pw)

    once, twice = times([rpg, rpp], cpp)
    put(once * inverse, rph, None)
    put(twice, None, cps)
    next_gram, next_first = exchange_and_times(rph, cps, [([rph], cpp), ([rph], cps)])
    put(next_gram, rpn, None)
    put(next_first, None, cpw)
    (next_second,) = exchange_and_times(rpn, cpw, [([rpn], cpw)])
    whole = (gain * root) * (first_coef * cube[...] + second_coef * next_first + third_coef * next_second)
    qi[z, x] = whole.astype(BF)

    sums_base = comm.next_recv
    for core in range(nc):

        @pl.when(c == core)
        def _():
            comm.next_recv = sums_base
            a1, a2 = ("z", "x") if core == 0 else ("x", "z")
            if n[a1] == 1:
                a1, a2 = a2, a1

            def slot(i1, i2, h):
                iz, ix = (i1, i2) if a1 == "z" else (i2, i1)
                return two_halves(qi.at[iz, ix], h, half_rows)

            together(tree(comm, me, n, a1, a2, slot, lambda d1, d2: None))
            comm.drain()

    comm.next_recv = comm.most_recv

    def product(side):
        def step(k, total):
            left = qi[k].reshape(rows_half, pw)
            right = xc[side, k // per_block, pl.ds(pl.multiple_of(k % per_block * pw, pw), pw)]
            return total + jnp.dot(left, right, preferred_element_type=F32)

        return lax.fori_loop(0, nz, step, jnp.zeros((rows_half, columns), F32)).astype(BF)

    if nc > 1:
        swap[0] = product(1 - c)
        index = comm.start(swap.at[0], swap.at[1], "c", 1 - c)
    o_ref[pl.ds(pl.multiple_of(c * rows_half, rows_half), rows_half)] = product(c)
    if nc > 1:
        comm.wait(swap.at[1], index, "c", 1 - c)
        o_ref[pl.ds(pl.multiple_of((1 - c) * rows_half, rows_half), rows_half)] = swap[1]
        comm.drain()
    for count, send, axis in unsent:
        comm.wait_sent(rpg.at[pl.ds(0, count)] if count < nz else blocks(count), send, axis, around(me[axis], 1, n[axis]))


def update_call(n, gain, x):
    nz, nx, nc, ny = n["z"], n["x"], n["c"], n["y"]
    rows_block, columns = x.shape
    rows = rows_block * ny
    ph, pw = rows // (ny * nc * nx), rows // nz
    row_panel = pltpu.VMEM((nz, ph, pw), BF)
    column_panel = pltpu.VMEM((ny, nc, nx, ph, pw), BF)
    hops_z, hops_x = max(nz // 2, 1), max(nx // 2, 1)
    tiles = 2 + ny + nx + nc
    return pl.pallas_call(
        lambda *refs: kernel(n, gain, *refs),
        out_shape=jax.ShapeDtypeStruct(x.shape, BF),
        in_specs=[pl.BlockSpec(memory_space=pltpu.VMEM)],
        out_specs=pl.BlockSpec(memory_space=pltpu.VMEM),
        scratch_shapes=[
            pltpu.VMEM((nc, ny, rows_block, columns), BF),
            pltpu.VMEM((nz, nx, ph, pw), BF),
            pltpu.VMEM((2, hops_z, nx, ph, pw), BF),
            pltpu.VMEM((2, hops_x, nz, ph, pw), BF),
            pltpu.VMEM((nz - 1, ph, pw), BF),
            pltpu.VMEM((nx - 1, ph, pw), BF),
            pltpu.VMEM((ph, pw), F32),
            pltpu.VMEM((ph, pw), F32),
            pltpu.VMEM((2, ph, pw), F32),
            row_panel, column_panel, row_panel, column_panel, row_panel, column_panel,
            row_panel, column_panel, row_panel, column_panel,
            pltpu.VMEM((nz, nx, ph, pw), BF),
            pltpu.VMEM((2, rows_block // nc, columns), BF),
            pltpu.VMEM((tiles, 8, 128), F32),
            pltpu.VMEM((8, 128), F32),
            pltpu.SemaphoreType.DMA((80,)),
            pltpu.SemaphoreType.DMA((300,)),
            pltpu.SemaphoreType.DMA,
        ],
        compiler_params=pltpu.CompilerParams(
            collective_id=0, has_side_effects=True, vmem_limit_bytes=48 * 1024 * 1024
        ),
    )(x)


def per_device(grad, momentum):
    new_momentum = momentum_beta * momentum + grad.astype(F32)
    iterate = (grad.astype(F32) + momentum_beta * new_momentum).astype(BF)
    update = update_call(SIZES, shape_gain * math.sqrt(max(R, C)), iterate)
    return (update, new_momentum)


def solution(mesh):
    devices = mesh.devices.reshape(SIZES["z"], SIZES["x"], SIZES["c"], SIZES["y"])
    split = Mesh(devices, (AX["z"], AX["x"], AX["c"], AX["y"]))
    mats = (AX["z"], AX["x"], AX["c"])
    return jax.shard_map(
        per_device,
        mesh=split,
        in_specs=(P(AX["y"], mats), P(AX["y"], mats)),
        out_specs=(P(AX["y"], mats), P(AX["y"], mats)),
        check_vma=False,
    )
```

time: 182 us -> 156 us (0.86)
  Pallas kernels: 178 us -> 152 us
    pallas_call x1, Pallas kernels: 178 us -> 152 us  [update_call(): pl.pallas_call(lambda *refs: kernel(n, gain, *refs), out_shape=jax.ShapeD...]
where the time goes in v2:
time: 156 us
  Pallas kernels  152 us (97%)
  other arithmetic  2.28 us (1%)
    pallas_call x1, Pallas kernels, update_call(): pl.pallas_call(lambda *refs: kernel(n, gain, *refs), out_shape=jax.ShapeD...  152 us

profile of v2, /device:TPU:1, one launch (start us, length us, event | category | flops | bytes accessed | tf_op | source)
XLA Modules:
  0.0 155.6 jit_solution(5623474913809354387)
XLA Ops:
  0.6 2.3 %fusion = (bf16[768,256]{1,0:T(8,128)(2,1)S(1)}, f32[768,256]{1,0:T(8,128)}) fusion(bf16[768,256]{1,0:T(8,128)(2,1)} %param.2, f32[768,256]{1,0:T(8,128)} %param.3), kind=kLoop, calls=%fused_computation.2 | loop fusion | flops 1179648 | bytes 2359296 | tf_op jit(solution)/shard_map/convert_element_type | solution.py:594
  2.9 151.9 %shard_map.41 = bf16[768,256]{1,0:T(8,128)(2,1)S(1)} custom-call(bf16[768,256]{1,0:T(8,128)(2,1)S(1)} %get-tuple-element.2.refs_0_), custom_call_target="tpu_custom_call" | custom-call | tf_op jit(solution)/shard_map/pallas_call | solution.py:561
  154.8 0.7 copy.5

commit v3 on v2

--- a/solution.py
+++ b/solution.py
@@ -181,7 +181,7 @@
 
 def kernel(
     n, gain, x_ref, o_ref, xc, part, z1, x1, z2, x2, gram, cube, sums, rpg, cpg, rp2, cp2, rpp, cpp, rph, cps, rpn, cpw,
-    qi, swap, edge, peaks, send_sems, recv_sems, local_sem,
+    qi, product, swap, edge, peaks, send_sems, recv_sems, local_sem,
 ):
     nz, nx, nc, ny = n["z"], n["x"], n["c"], n["y"]
     me = {a: (lax.axis_index(AX[a]) if n[a] > 1 else 0) for a in "zxcy"}
@@ -510,41 +510,152 @@
     whole = (gain * root) * (first_coef * cube[...] + second_coef * next_first + third_coef * next_second)
     qi[z, x] = whole.astype(BF)
 
-    sums_base = comm.next_recv
+    def share_of(d):
+        k = around(z, d, nz)
+        left = qi[k].reshape(rows_half, pw)
+        for side in range(nc):
+            product[side] += jnp.dot(left, right_rows(around(c, 1 - side, nc), k), preferred_element_type=F32)
+
+    product[...] = jnp.zeros(product.shape, F32)
+    base_recv, base_send = comm.next_recv, comm.next_send
+
+    def q(d, e, h=None):
+        ref = qi.at[around(z, d, nz), around(x, e, nx)]
+        return two_halves(ref, h, half_rows)
+
+    def to_z(d, e, way, index, send, h=None):
+        comm.start(q(d, e, h), q(d, e, h), "z", around(z, way, nz), index, send)
+
+    def to_x(d, e, way, index, send, h=None):
+        comm.start(q(d, e, h), q(d, e, h), "x", around(x, way, nx), index, send)
+
+    def take(count, index, axis):
+        comm.wait(blocks(count), index, axis, around(me[axis], 1, n[axis]))
+
+    def gather_z_first():
+        z_send, x_send = comm.send_index(), comm.send_index()
+        far, near, three, four = {w: comm.recv_index() for w in (1, -1)}, comm.recv_index(), comm.recv_index(), comm.recv_index()
+        groups = {0: [0], 1: [-1, 1], 2: [-2, 2], 3: [-3, 3], 4: [4]}
+        hop = {(g, w): comm.recv_index() for g in groups for w in (1, -1)}
+        last = {g: comm.recv_index() for g in groups}
+
+        def spread(g, ds):
+            for d in ds:
+                for w in (1, -1):
+                    to_x(d, 0, w, hop[g, w], x_send)
+                if g == 4:
+                    to_x(d, 0, 2, last[g], x_send)
+
+        def pass_on(g):
+            for w in (1, -1):
+                take(len(groups[g]), hop[g, w], "x")
+                if g < 4:
+                    for d in groups[g]:
+                        to_x(d, -w, w, last[g], x_send, 0 if w > 0 else 1)
+
+        def finish(g):
+            take(len(groups[g]), last[g], "x")
+            for d in groups[g]:
+                share_of(d)
+
+        for w in (1, -1):
+            to_z(0, 0, 2 * w, far[w], z_send)
+        for w in (1, -1):
+            to_z(0, 0, w, near, z_send)
+        spread(0, [0])
+        for w in (1, -1):
+            take(1, far[w], "z")
+            to_z(-2 * w, 0, w, three, z_send)
+            to_z(-2 * w, 0, 2 * w, four, z_send, 0 if w > 0 else 1)
+            spread(2, [-2 * w])
+        take(2, near, "z")
+        spread(1, groups[1])
+        pass_on(0)
+        take(2, three, "z")
+        spread(3, groups[3])
+        take(1, four, "z")
+        spread(4, [4])
+        pass_on(2)
+        pass_on(1)
+        finish(0)
+        pass_on(3)
+        finish(2)
+        finish(1)
+        pass_on(4)
+        finish(3)
+        finish(4)
+        take_sent(7, z_send, "z")
+        take_sent(24, x_send, "x")
+
+    def gather_x_first():
+        x_send, z_send = comm.send_index(), comm.send_index()
+        near_x, far_x = comm.recv_index(), comm.recv_index()
+        groups = {0: [0], 1: [-1, 1]}
+        chain = {(g, h, w): comm.recv_index() for g in groups for h in range(1, 4) for w in (1, -1)}
+        chain.update({(g, 4, w): k for g in groups for k in [comm.recv_index()] for w in (1, -1)})
+        far, near, three, four = {w: comm.recv_index() for w in (1, -1)}, comm.recv_index(), comm.recv_index(), comm.recv_index()
+
+        def go(g, h):
+            for w in (1, -1):
+                if h > 1:
+                    take(len(groups[g]), chain[g, h - 1, w], "z")
+                for e in groups[g]:
+                    to_z(-w * (h - 1), e, w, chain[g, h, w], z_send, None if h < 4 else 0 if w > 0 else 1)
+
+        to_x(0, 0, 2, far_x, x_send)
+        for w in (1, -1):
+            to_x(0, 0, w, near_x, x_send)
+        go(0, 1)
+        take(2, near_x, "x")
+        go(1, 1)
+        take(1, far_x, "x")
+        for w in (1, -1):
+            to_z(0, 2, 2 * w, far[w], z_send)
+        for w in (1, -1):
+            to_z(0, 2, w, near, z_send)
+        go(0, 2)
+        share_of(0)
+        go(1, 2)
+        go(0, 3)
+        for w in (1, -1):
+            take(1, far[w], "z")
+            to_z(-2 * w, 2, w, three, z_send)
+            to_z(-2 * w, 2, 2 * w, four, z_send, 0 if w > 0 else 1)
+        go(1, 3)
+        take(2, near, "z")
+        share_of(-1)
+        share_of(1)
+        go(0, 4)
+        share_of(-2)
+        share_of(2)
+        go(1, 4)
+        take(2, three, "z")
+        share_of(-3)
+        share_of(3)
+        take(1, four, "z")
+        take(1, chain[0, 4, 1], "z")
+        take(2, chain[1, 4, 1], "z")
+        share_of(4)
+        take_sent(3, x_send, "x")
+        take_sent(28, z_send, "z")
+
+    def take_sent(count, send, axis):
+        comm.wait_sent(blocks(count), send, axis, around(me[axis], 1, n[axis]))
+
     for core in range(nc):
 
         @pl.when(c == core)
         def _():
-            comm.next_recv = sums_base
-            a1, a2 = ("z", "x") if core == 0 else ("x", "z")
-            if n[a1] == 1:
-                a1, a2 = a2, a1
-
-            def slot(i1, i2, h):
-                iz, ix = (i1, i2) if a1 == "z" else (i2, i1)
-                return two_halves(qi.at[iz, ix], h, half_rows)
-
-            together(tree(comm, me, n, a1, a2, slot, lambda d1, d2: None))
-            comm.drain()
+            comm.next_recv, comm.next_send = base_recv, base_send
+            (gather_z_first if core == 0 else gather_x_first)()
 
     comm.next_recv = comm.most_recv
-
-    def product(side):
-        def step(k, total):
-            left = qi[k].reshape(rows_half, pw)
-            right = xc[side, k // per_block, pl.ds(pl.multiple_of(k % per_block * pw, pw), pw)]
-            return total + jnp.dot(left, right, preferred_element_type=F32)
-
-        return lax.fori_loop(0, nz, step, jnp.zeros((rows_half, columns), F32)).astype(BF)
-
-    if nc > 1:
-        swap[0] = product(1 - c)
-        index = comm.start(swap.at[0], swap.at[1], "c", 1 - c)
-    o_ref[pl.ds(pl.multiple_of(c * rows_half, rows_half), rows_half)] = product(c)
-    if nc > 1:
-        comm.wait(swap.at[1], index, "c", 1 - c)
-        o_ref[pl.ds(pl.multiple_of((1 - c) * rows_half, rows_half), rows_half)] = swap[1]
-        comm.drain()
+    swap[0] = product[0].astype(BF)
+    index = comm.start(swap.at[0], swap.at[1], "c", 1 - c)
+    o_ref[pl.ds(top, rows_half)] = product[1].astype(BF)
+    comm.wait(swap.at[1], index, "c", 1 - c)
+    o_ref[pl.ds(pl.multiple_of((1 - c) * rows_half, rows_half), rows_half)] = swap[1]
+    comm.drain()
     for count, send, axis in unsent:
         comm.wait_sent(rpg.at[pl.ds(0, count)] if count < nz else blocks(count), send, axis, around(me[axis], 1, n[axis]))
 
@@ -576,6 +687,7 @@
             row_panel, column_panel, row_panel, column_panel, row_panel, column_panel,
             row_panel, column_panel, row_panel, column_panel,
             pltpu.VMEM((nz, nx, ph, pw), BF),
+            pltpu.VMEM((nc, rows_block // nc, columns), F32),
             pltpu.VMEM((2, rows_block // nc, columns), BF),
             pltpu.VMEM((tiles, 8, 128), F32),
             pltpu.VMEM((8, 128), F32),

time: 156 us -> 150 us (0.962)
  Pallas kernels: 152 us -> 146 us
    pallas_call x1, Pallas kernels: 152 us -> 146 us  [update_call(): pl.pallas_call(lambda *refs: kernel(n, gain, *refs), out_shape=jax.ShapeD...]
where the time goes in v3:
time: 150 us
  Pallas kernels  146 us (97%)
  other arithmetic  2.28 us (2%)
    pallas_call x1, Pallas kernels, update_call(): pl.pallas_call(lambda *refs: kernel(n, gain, *refs), out_shape=jax.ShapeD...  146 us

profile of v3, /device:TPU:1, one launch (start us, length us, event | category | flops | bytes accessed | tf_op | source)
XLA Modules:
  0.0 150.0 jit_solution(754454486040904820)
XLA Ops:
  0.6 2.3 %fusion = (bf16[768,256]{1,0:T(8,128)(2,1)S(1)}, f32[768,256]{1,0:T(8,128)}) fusion(bf16[768,256]{1,0:T(8,128)(2,1)} %param.2, f32[768,256]{1,0:T(8,128)} %param.3), kind=kLoop, calls=%fused_computation.2 | loop fusion | flops 1179648 | bytes 2359296 | tf_op jit(solution)/shard_map/convert_element_type | solution.py:706
  2.9 146.3 %shard_map.41 = bf16[768,256]{1,0:T(8,128)(2,1)S(1)} custom-call(bf16[768,256]{1,0:T(8,128)(2,1)S(1)} %get-tuple-element.2.refs_0_), custom_call_target="tpu_custom_call" | custom-call | tf_op jit(solution)/shard_map/pallas_call | solution.py:672
  149.2 0.7 copy.5

commit v4 on v3

--- a/solution.py
+++ b/solution.py
@@ -87,100 +87,8 @@
         self.open = []
 
 
-def ring_relay(comm, me, n, axis, slot, arrived):
-    size, s = n[axis], me[axis]
-    at = lambda d: around(s, d, size)
-    send = comm.send_index()
-    near, far = comm.recv_index(), {1: comm.recv_index(), -1: comm.recv_index()}
-    own = slot(s, None)
-    for way in (1, -1):
-        comm.start(own, own, axis, at(2 * way), far[way], send)
-    for way in (1, -1):
-        comm.start(own, own, axis, at(way), near, send)
-    yield
-    for way in (1, -1):
-        piece = slot(at(-2 * way), None)
-        comm.wait(piece, far[way], axis, at(-2 * way))
-        comm.start(piece, piece, axis, at(way), near, send)
-        half = slot(at(-2 * way), 0 if way > 0 else 1)
-        comm.start(half, half, axis, at(2 * way), near, send)
-    yield
-    arrived(near, send)
-
-
-def tree(comm, me, n, a1, a2, slot, arrived):
-    n1, n2 = n[a1], (n[a2] if a2 else 1)
-    s1, s2 = me[a1], (me[a2] if a2 else 0)
-    held = {}
-
-    def ref(d1, d2, h):
-        return slot(around(s1, d1, n1), around(s2, d2, n2), h)
-
-    def send(level, d1, d2, hop, way):
-        axis, size, s = (a1, n1, s1) if level == 1 else (a2, n2, s2)
-        half = None if hop < size // 2 else (0 if way > 0 else 1)
-        piece = ref(d1, d2, half)
-        index = comm.start(piece, piece, axis, around(s, way, size))
-        key = (1, d1 - way, d2, hop, way) if level == 1 else (2, d1, d2 - way, hop, way)
-        held[key] = (index, half)
-
-    def take(level, d1, d2, hop, way):
-        index, half = held.pop((level, d1, d2, hop, way))
-        axis, size, s = (a1, n1, s1) if level == 1 else (a2, n2, s2)
-        comm.wait(ref(d1, d2, half), index, axis, around(s, way, size))
-
-    def spread(d1):
-        if n2 > 1:
-            for way in (1, -1):
-                send(2, d1, 0, 1, way)
-
-    if n1 > 1:
-        for way in (1, -1):
-            send(1, 0, 0, 1, way)
-    spread(0)
-    arrived(0, 0)
-    yield
-    last1, last2 = n1 // 2, n2 // 2
-    for hop in range(1, last1 + last2 + 1):
-        if n1 > 1 and hop <= last1:
-            for way in (1, -1):
-                d1 = -hop * way
-                take(1, d1, 0, hop, way)
-                if hop < last1:
-                    send(1, d1, 0, hop + 1, way)
-                    spread(d1)
-                    arrived(d1, 0)
-            if hop == last1:
-                spread(last1)
-                arrived(last1, 0)
-        for t1 in range(last1 + 1):
-            t2 = hop - t1
-            if n2 == 1 or not 1 <= t2 <= last2:
-                continue
-            for d1 in [0] if t1 == 0 else [last1] if t1 == last1 else [-t1, t1]:
-                for way in (1, -1):
-                    d2 = -t2 * way
-                    take(2, d1, d2, t2, way)
-                    if t2 < last2:
-                        send(2, d1, d2, t2 + 1, way)
-                        arrived(d1, d2)
-                if t2 == last2:
-                    arrived(d1, last2)
-        yield
-
-
-def together(*walks):
-    walks = list(walks)
-    while walks:
-        for walk in list(walks):
-            try:
-                next(walk)
-            except StopIteration:
-                walks.remove(walk)
-
-
 def kernel(
-    n, gain, x_ref, o_ref, xc, part, z1, x1, z2, x2, gram, cube, sums, rpg, cpg, rp2, cp2, rpp, cpp, rph, cps, rpn, cpw,
+    n, gain, x_ref, o_ref, xc, part, z1, x1, z2, x2, gram, cube, sums, rpg, cpg, rp2, cp2, rp3, cpp, rph, rpn, cpn, rpw,
     qi, product, swap, edge, peaks, send_sems, recv_sems, local_sem,
 ):
     nz, nx, nc, ny = n["z"], n["x"], n["c"], n["y"]
@@ -194,36 +102,51 @@
     comm = Comm(send_sems, recv_sems)
 
     barrier = pltpu.get_barrier_semaphore()
-    peers = [(a, d) for a in "zxcy" for d in range(1, n[a])]
+    peers = [(a, d) for a in "zxcy" for d in range(1, n[a]) if a != "z" or d in (1, 2, nz - 2, nz - 1)]
     for a, d in peers:
         pl.semaphore_signal(barrier, inc=1, device_id={AX[a]: around(me[a], d, n[a])}, device_id_type=MESH)
     pl.semaphore_wait(barrier, len(peers))
 
-    parts = 2
-    share = rows_block // parts
-
-    def x_slot(i, q, h):
-        if h is None:
-            return xc.at[c, i, pl.ds(q * share, share)]
-        return xc.at[c, i, pl.ds(q * share + h * (share // 2), share // 2)]
-
     own = pltpu.make_async_copy(x_ref, xc.at[c, y], local_sem)
     own.start()
+    quarter = rows_block // 4
+    x_send, x_over_send, x_over = comm.send_index(), comm.send_index(), comm.recv_index()
+    came = {(w, k): comm.recv_index() for w in (1, -1) for k in range(5)}
+
+    def block(d, k, count=1):
+        return xc.at[c, around(y, d, ny), pl.ds(k * quarter, count * quarter)]
+
+    def to_y(ref, dst, w, k):
+        comm.start(ref, dst, "y", around(y, w, ny), came[w, k], x_send)
+
+    def from_y(w, k, ref):
+        comm.wait(ref, came[w, k], "y", around(y, -w, ny))
+
+    def to_other(d, k, count):
+        comm.start(block(d, k, count), block(d, k, count), "c", 1 - c, x_over, x_over_send)
+
+    for k in range(4):
+        for w, q in ((1, k), (-1, 3 - k)):
+            to_y(x_ref.at[pl.ds(q * quarter, quarter)], block(0, q), w, min(k, 2))
+    comm.start(x_ref, xc.at[c, y], "c", 1 - c, x_over, x_over_send)
+    for k in range(2):
+        for w, q in ((1, k), (-1, 3 - k)):
+            from_y(w, k, block(-w, q))
+            to_y(block(-w, q), block(-w, q), w, 3 + k)
+    to_other(-1, 0, 2)
+    to_other(1, 2, 2)
+    from_y(1, 2, block(-1, 2, 2))
+    to_other(-1, 2, 2)
+    from_y(-1, 2, block(1, 0, 2))
+    to_other(1, 0, 2)
+    for k in range(2):
+        for w, q in ((1, k), (-1, 3 - k)):
+            from_y(w, 3 + k, block(2, q))
+            to_other(2, q, 1)
     own.wait()
-    to_partner = {}
-
-    def x_arrived(q):
-        def done(d, _):
-            if nc > 1:
-                ref = x_slot(around(y, d, ny), q, None)
-                to_partner[q, d % ny] = comm.start(ref, ref, "c", 1 - c)
-
-        return done
-
-    together(*(tree(comm, me, n, "y", None, lambda i, _, h, q=q: x_slot(i, q, h), x_arrived(q)) for q in range(parts)))
-    for (q, d), index in to_partner.items():
-        comm.wait(xc.at[1 - c, around(y, d, ny), pl.ds(q * share, share)], index, "c", 1 - c)
-    comm.drain()
+    comm.wait(xc.at[1 - c], x_over, "c", 1 - c)
+    comm.wait_sent(xc.at[c, pl.ds(0, 3)], x_send, "y", around(y, 1, ny))
+    comm.wait_sent(xc.at[c], x_over_send, "c", 1 - c)
 
     per_block = rows_block // pw
     top = pl.multiple_of(c * rows_half, rows_half)
@@ -253,12 +176,12 @@
             total += other[...].astype(F32)
         return total
 
-    def plane_sum(axis, piece, landing, chunks, prepare, across, final_landing):
+    def plane_sum(axis, piece, landing, chunks, prepare, finish):
         size, s = n[axis], me[axis]
         last = size // 2
         halves = {1: chunks[: len(chunks) // 2], -1: chunks[len(chunks) // 2 :]}
         index = {}
-        send, final_send, final = comm.send_index(), comm.send_index(), comm.recv_index()
+        send = comm.send_index()
 
         def go(way, hop, e):
             index[way, hop, e] = comm.recv_index()
@@ -288,19 +211,59 @@
                         ref[...] = plus(ref, come(way, hop - 1, e)).astype(BF)
                         go(way, hop, e)
         prepare(s)
-        order = [e for pair in zip(halves[1], halves[-1]) for e in pair]
-        for e in order:
-            ref = piece(s, e)
-            total = plus(ref, come(1, last, e), come(-1, last, e))
+
+        def summed(e):
+            return plus(piece(s, e), come(1, last, e), come(-1, last, e))
+
+        finish(summed, lambda e: piece(s, e))
+        comm.wait_sent(blocks((size - 1) * len(chunks)), send, axis, around(s, 1, size))
+
+    def straight_to_x(summed, kept):
+        index, send = comm.recv_index(), comm.send_index()
+        for e in (2, 3, 1, 0):
             if e == 0:
-                gram[...] = total
+                gram[...] = summed(e)
             else:
-                ref[...] = total.astype(BF)
-                comm.start(ref, final_landing.at[e - 1], across, around(me[across], e, n[across]), final, final_send)
-        comm.wait(final_landing, final, across, around(me[across], 1, n[across]))
-        gram[...] = plus(gram, *(final_landing.at[k] for k in range(n[across] - 1)))
-        comm.wait_sent(blocks((size - 1) * len(chunks)), send, axis, around(s, 1, size))
-        comm.wait_sent(final_landing, final_send, across, around(me[across], 1, n[across]))
+                kept(e)[...] = summed(e).astype(BF)
+                comm.start(kept(e), x2.at[e - 1], "x", around(x, e, nx), index, send)
+        comm.wait(x2, index, "x", around(x, 1, nx))
+        gram[...] = plus(gram, *(x2.at[k] for k in range(nx - 1)))
+        comm.wait_sent(x2, send, "x", around(x, 1, nx))
+
+    def two_hops_to_z(summed, kept):
+        send, end = comm.send_index(), comm.recv_index()
+        three = {w: comm.recv_index() for w in (1, -1)}
+        four = {w: comm.recv_index() for w in (1, -1)}
+
+        def go(ref, slot, index, way):
+            comm.start(ref, slot, "z", around(z, way, nz), index, send)
+
+        for e in (4, 3, 5, 6, 2, 1, 7):
+            kept(e)[...] = summed(e).astype(BF)
+            if e == 4:
+                for w in (1, -1):
+                    h = 0 if w > 0 else 1
+                    go(two_halves(kept(4), h, half_rows), two_halves(z2.at[2], h, half_rows), four[w], 2 * w)
+            elif e in (3, 5):
+                w = 1 if e == 3 else -1
+                go(kept(e), z2.at[0 if w > 0 else 1], three[w], w)
+            elif e in (1, 7):
+                w = 1 if e == 1 else -1
+                go(kept(e), z2.at[3 if w > 0 else 4], end, w)
+        gram[...] = summed(0)
+        for w in (1, -1):
+            mid = kept(2 * w % nz)
+            slot, h = z2.at[0 if w > 0 else 1], 0 if w > 0 else 1
+            comm.wait(slot, three[w], "z", around(z, -w, nz))
+            mid[...] = plus(mid, slot).astype(BF)
+            half = two_halves(z2.at[2], h, half_rows)
+            comm.wait(half, four[w], "z", around(z, -2 * w, nz))
+            part_of = two_halves(mid, h, half_rows)
+            part_of[...] = plus(part_of, half).astype(BF)
+            go(mid, z2.at[5 if w > 0 else 6], end, 2 * w)
+        comm.wait(z2.at[pl.ds(3, 4)], end, "z", around(z, 1, nz))
+        gram[...] = plus(gram, *(z2.at[k] for k in range(3, 7)))
+        comm.wait_sent(z2, send, "z", around(z, 1, nz))
 
     def two_halves(ref, h, length):
         return ref if h is None else ref.at[pl.ds(h * length, length)]
@@ -318,101 +281,154 @@
             if core == 0:
                 plane_sum(
                     "z", lambda d, e: part.at[d, around(x, e, nx)], lambda way, hop, e: z1.at[int(way > 0), hop - 1, e],
-                    [2, 1, 3, 0], part_columns, "x", x2,
+                    [2, 1, 3, 0], part_columns, straight_to_x,
                 )
             else:
                 plane_sum(
                     "x", lambda d, e: part.at[around(z, e, nz), d], lambda way, hop, e: x1.at[int(way > 0), hop - 1, e],
-                    [4, 5, 2, 7, 3, 6, 1, 0], part_rows, "z", z2,
+                    [4, 5, 2, 7, 3, 6, 1, 0], part_rows, two_hops_to_z,
                 )
 
     comm.next_recv = comm.most_recv
 
     unsent = []
 
-    def panels(rp, cp, half_done, peak=False):
+    def take(count, index, axis):
+        comm.wait(blocks(count), index, axis, around(me[axis], 1, n[axis]))
+
+    class Rows:
+        def __init__(self, rp):
+            self.rp, self.send = rp, comm.send_index()
+            self.near, self.far = comm.recv_index(), {w: comm.recv_index() for w in (1, -1)}
+
+        def to(self, d, way, index, h=None):
+            ref = two_halves(self.rp.at[around(z, d, nz)], h, half_rows)
+            comm.start(ref, ref, "z", around(z, way, nz), index, self.send)
+
+        def begin(self):
+            for w in (1, -1):
+                self.to(0, 2 * w, self.far[w])
+            for w in (1, -1):
+                self.to(0, w, self.near)
+
+        def forward(self):
+            for w in (1, -1):
+                take(1, self.far[w], "z")
+                self.to(-2 * w, w, self.near)
+                self.to(-2 * w, 2 * w, self.near, 0 if w > 0 else 1)
+
+        def finish(self):
+            take(nz - 3, self.near, "z")
+
+    class Columns:
+        def __init__(self, core, cp):
+            self.core, self.cp = core, cp
+            self.a1, self.a2 = ("y", "x") if core == 0 else ("x", "y")
+            self.over, self.send_over, self.send = comm.recv_index(), comm.send_index(), comm.send_index()
+            self.near, self.far, self.last = comm.recv_index(), comm.recv_index(), comm.recv_index()
+            self.hop = {(w, k): comm.recv_index() for w in (1, -1) for k in range(3)}
+
+        def at1(self, d):
+            return around(me[self.a1], d, n[self.a1])
+
+        def at2(self, d):
+            return around(me[self.a2], d, n[self.a2])
+
+        def spot(self, d1, d2, h=None):
+            iy, ix = (self.at1(d1), self.at2(d2)) if self.a1 == "y" else (self.at2(d2), self.at1(d1))
+            return two_halves(self.cp.at[iy, self.core, ix], h, half_rows)
+
+        def to_partner(self, d2):
+            ref = self.cp.at[:, self.core, self.at2(d2)] if self.a1 == "y" else self.cp.at[self.at2(d2), self.core]
+            comm.start(ref, ref, "c", 1 - c, self.over, self.send_over)
+
+        def spread(self, d1, k):
+            ref = self.spot(d1, 0)
+            for w in (1, -1):
+                comm.start(ref, ref, self.a2, self.at2(w), self.hop[w, k], self.send)
+            if d1 == 2:
+                comm.start(ref, ref, self.a2, self.at2(2), self.last, self.send)
+
+        def pass_on(self, w, d1s):
+            for d1 in d1s:
+                half = self.spot(d1, -w, 0 if w > 0 else 1)
+                comm.start(half, half, self.a2, self.at2(w), self.last, self.send)
+
+        def begin(self):
+            own = self.spot(0, 0)
+            comm.start(own, own, self.a1, self.at1(2), self.far, self.send)
+            for w in (1, -1):
+                comm.start(own, own, self.a1, self.at1(w), self.near, self.send)
+
+        def first(self):
+            take(2, self.near, self.a1)
+            self.spread(-1, 1)
+            self.spread(1, 1)
+            for w in (1, -1):
+                take(1, self.hop[w, 0], self.a2)
+                self.pass_on(w, [0])
+            take(1, self.far, self.a1)
+            self.spread(2, 2)
+            self.to_partner(0)
+
+        def middle(self):
+            for w in (1, -1):
+                take(2, self.hop[w, 1], self.a2)
+                self.pass_on(w, [-1, 1])
+            for w in (1, -1):
+                take(1, self.hop[w, 2], self.a2)
+                self.to_partner(-w)
+
+        def end(self):
+            take(4, self.last, self.a2)
+            self.to_partner(2)
+
+        def finish(self):
+            take(16, self.over, "c")
+
+    def exchange(rp, cp, half_done=None, rp_next=None, next_piece=None, meanwhile=None, peak=False):
         base_recv, base_send = comm.next_recv, comm.next_send
         for core in range(nc):
 
             @pl.when(c == core)
             def _():
                 comm.next_recv, comm.next_send = base_recv, base_send
-                over, peak_over = comm.recv_index(), comm.recv_index()
-                send, send_over = comm.send_index(), comm.send_index()
-                a1, a2 = ("y", "x") if core == 0 else ("x", "y")
-                n1, n2 = n[a1], n[a2]
-                at1, at2 = (lambda d: around(me[a1], d, n1)), (lambda d: around(me[a2], d, n2))
-
-                def spot(d1, d2, h=None):
-                    iy, ix = (at1(d1), at2(d2)) if a1 == "y" else (at2(d2), at1(d1))
-                    return cp.at[iy, core, ix] if h is None else cp.at[iy, core, ix, pl.ds(h * half_rows, half_rows)]
-
-                def group(d2):
-                    return cp.at[:, core, at2(d2)] if a1 == "y" else cp.at[at2(d2), core]
-
-                def to_partner(d2):
-                    comm.start(group(d2), group(d2), "c", 1 - c, over, send_over)
-
-                near1, far1, last = comm.recv_index(), comm.recv_index(), comm.recv_index()
-                hop2 = {(way, k): comm.recv_index() for way in (1, -1) for k in range(3)}
-
-                def spread(d1, k):
-                    for way in (1, -1):
-                        comm.start(spot(d1, 0), spot(d1, 0), a2, at2(way), hop2[way, k], send)
-                    if d1 == 2:
-                        comm.start(spot(d1, 0), spot(d1, 0), a2, at2(2), last, send)
-
-                def pass_on(way, d1s):
-                    for d1 in d1s:
-                        half = spot(d1, -way, 0 if way > 0 else 1)
-                        comm.start(half, half, a2, at2(way), last, send)
-
-                def several(count):
-                    return blocks(count)
-
-                z_left = []
-                z_walk = ring_relay(
-                    comm, me, n, "z", lambda i, h: two_halves(rp.at[i], h, half_rows), lambda *left: z_left.append(left)
-                )
-                own = spot(0, 0)
-                comm.start(own, own, a1, at1(2), far1, send)
-                for way in (1, -1):
-                    comm.start(own, own, a1, at1(way), near1, send)
-                next(z_walk)
-                spread(0, 0)
-                peak_walk = largest(peak_over) if peak else iter(())
+                columns, rows = Columns(core, cp), Rows(rp)
+                peak_walk = largest(comm.recv_index()) if peak else iter(())
+                columns.begin()
+                rows.begin()
+                columns.spread(0, 0)
                 next(peak_walk, None)
-
-                comm.wait(several(2), near1, a1, at1(1))
-                spread(-1, 1)
-                spread(1, 1)
-                for way in (1, -1):
-                    comm.wait(own, hop2[way, 0], a2, at2(way))
-                    pass_on(way, [0])
-                comm.wait(own, far1, a1, at1(2))
-                spread(2, 2)
-                to_partner(0)
-                next(z_walk)
-                next(peak_walk, None)
-                for way in (1, -1):
-                    comm.wait(several(2), hop2[way, 1], a2, at2(way))
-                    pass_on(way, [-1, 1])
-                for way in (1, -1):
-                    comm.wait(own, hop2[way, 2], a2, at2(way))
-                    to_partner(-way)
-                next(peak_walk, None)
-                next(z_walk, None)
-                comm.wait(several(4), last, a2, at2(1))
-                to_partner(2)
-                ((near, z_send),) = z_left
-                comm.wait(rp.at[pl.ds(0, nz - 3)], near, "z", around(z, 1, nz))
-                next(peak_walk, None)
-                half_done()
-                comm.wait(several(16), over, "c", 1 - c)
+                if rp_next is None:
+                    columns.first()
+                    rows.forward()
+                    columns.middle()
+                    rows.finish()
+                    columns.end()
+                    half_done()
+                    columns.finish()
+                else:
+                    rows.forward()
+                    columns.first()
+                    next(peak_walk, None)
+                    rows.finish()
+                    rp_next[z] = next_piece().astype(BF)
+                    next_rows = Rows(rp_next)
+                    next_rows.begin()
+                    columns.middle()
+                    next(peak_walk, None)
+                    next_rows.forward()
+                    columns.end()
+                    next(peak_walk, None)
+                    columns.finish()
+                    meanwhile()
+                    next_rows.finish()
                 if core == 0:
-                    unsent.append((7, z_send, "z"))
-                    unsent.append((15, send, "y"))
-                    unsent.append((16, send_over, "c"))
+                    unsent.append((7, rows.send, "z"))
+                    unsent.append((15, columns.send, "y"))
+                    unsent.append((16, columns.send_over, "c"))
+                    if rp_next is not None:
+                        unsent.append((7, next_rows.send, "z"))
 
         comm.next_recv = comm.most_recv
 
@@ -448,66 +464,69 @@
             totals = tuple(jnp.zeros((ph, pw), F32) for _ in rps)
         return lax.fori_loop(0, nz if core is None else nz // nc, step, totals)
 
-    def exchange_and_times(rp, cp, pairs, peak=False):
-        def half_done():
-            at = 0
-            for rps, right in pairs:
-                for total in times(rps, right, c):
-                    sums[at] = total
-                    at += 1
-
-        panels(rp, cp, half_done, peak)
-        results, at = [], 0
-        for rps, right in pairs:
-            results += times(rps, right, 1 - c, tuple(sums[at + k] for k in range(len(rps))))
-            at += len(rps)
-        return results
-
     def with_identity(value, row, column, scale):
         rows = lax.broadcasted_iota(jnp.int32, value.shape, 0) + row
         across = lax.broadcasted_iota(jnp.int32, value.shape, 1) + column
         return value + jnp.where(rows == across, scale, 0.0)
 
     put(gram[...], rpg, cpg)
-    (square,) = exchange_and_times(rpg, cpg, [([rpg], cpg)])
+
+    def first_half():
+        (sums[...],) = times([rpg], cpg, c)
+
+    exchange(rpg, cpg, first_half)
 
     def sizes(k, total):
         return total + jnp.abs(rpg[k].astype(F32))
 
     row_sums = jnp.sum(lax.fori_loop(0, nz, sizes, jnp.zeros((ph, pw), F32)), axis=1, keepdims=True)
     edge[0] = jnp.broadcast_to(jnp.max(row_sums, axis=0, keepdims=True), edge.shape[1:])
+    (square,) = times([rpg], cpg, 1 - c, (sums[...],))
+    sums[...] = square
     put(square, rp2, cp2)
-    panels(rp2, cp2, lambda: None, peak=True)
-
-    bound = jnp.max(jnp.max(peaks[...], axis=1, keepdims=True), axis=0, keepdims=True) + epsilon
-    inverse = 1.0 / bound
-    root = lax.rsqrt(bound)
-
-    def mix(once, twice, row, column):
+
+    def scales():
+        bound = jnp.max(jnp.max(peaks[...], axis=1, keepdims=True), axis=0, keepdims=True) + epsilon
+        return 1.0 / bound, lax.rsqrt(bound)
+
+    def mix(once, twice, inverse, row, column):
         value = second_coef * (once.astype(F32) * inverse) + third_coef * (twice.astype(F32) * inverse * inverse)
         return with_identity(value, row, column, first_coef)
 
-    def mix_rows(k, carry):
-        rpp[k] = mix(rpg[k], rp2[k], mine * ph, k * pw).astype(BF)
+    def mixed_columns():
+        inverse, _ = scales()
+
+        def step(k, carry):
+            at = (k // (nc * nx), k // nx % nc, k % nx)
+            cpp[at] = mix(cpg[at], cp2[at], inverse, k * ph, z * pw).astype(BF)
+            return carry
+
+        lax.fori_loop(0, ny * nc * nx, step, 0)
+        cube[...] = mix(gram[...], sums[...], inverse, mine * ph, z * pw)
+
+    exchange(rp2, cp2, None, rp3, lambda: times([rp2], cpg)[0], mixed_columns, peak=True)
+
+    inverse, root = scales()
+
+    def product_rows(k, carry):
+        once = rpg[k].astype(F32) * inverse
+        twice = rp2[k].astype(F32) * inverse * inverse
+        thrice = rp3[k].astype(F32) * inverse * inverse * inverse
+        rph[k] = (first_coef * once + second_coef * twice + third_coef * thrice).astype(BF)
         return carry
 
-    def mix_columns(k, carry):
-        at = (k // (nc * nx), k // nx % nc, k % nx)
-        cpp[at] = mix(cpg[at], cp2[at], k * ph, z * pw).astype(BF)
-        return carry
-
-    lax.fori_loop(0, nz, mix_rows, 0)
-    lax.fori_loop(0, ny * nc * nx, mix_columns, 0)
-    cube[...] = mix(gram[...], square, mine * ph, z * pw)
-
-    once, twice = times([rpg, rpp], cpp)
-    put(once * inverse, rph, None)
-    put(twice, None, cps)
-    next_gram, next_first = exchange_and_times(rph, cps, [([rph], cpp), ([rph], cps)])
-    put(next_gram, rpn, None)
-    put(next_first, None, cpw)
-    (next_second,) = exchange_and_times(rpn, cpw, [([rpn], cpw)])
-    whole = (gain * root) * (first_coef * cube[...] + second_coef * next_first + third_coef * next_second)
+    lax.fori_loop(0, nz, product_rows, 0)
+    (next_gram,) = times([rph], cpp)
+    put(next_gram, rpn, cpn)
+
+    def next_first():
+        (value,) = times([rpn], cpp)
+        sums[...] = value
+        return value
+
+    exchange(rpn, cpn, None, rpw, next_first, lambda: None)
+    (next_second,) = times([rpw], cpn)
+    whole = (gain * root) * (first_coef * cube[...] + second_coef * sums[...] + third_coef * next_second)
     qi[z, x] = whole.astype(BF)
 
     def share_of(d):
@@ -528,9 +547,6 @@
 
     def to_x(d, e, way, index, send, h=None):
         comm.start(q(d, e, h), q(d, e, h), "x", around(x, way, nx), index, send)
-
-    def take(count, index, axis):
-        comm.wait(blocks(count), index, axis, around(me[axis], 1, n[axis]))
 
     def gather_z_first():
         z_send, x_send = comm.send_index(), comm.send_index()
@@ -683,9 +699,9 @@
             pltpu.VMEM((nx - 1, ph, pw), BF),
             pltpu.VMEM((ph, pw), F32),
             pltpu.VMEM((ph, pw), F32),
-            pltpu.VMEM((2, ph, pw), F32),
+            pltpu.VMEM((ph, pw), F32),
             row_panel, column_panel, row_panel, column_panel, row_panel, column_panel,
-            row_panel, column_panel, row_panel, column_panel,
+            row_panel, row_panel, column_panel, row_panel,
             pltpu.VMEM((nz, nx, ph, pw), BF),
             pltpu.VMEM((nc, rows_block // nc, columns), F32),
             pltpu.VMEM((2, rows_block // nc, columns), BF),

time: 150 us -> 141 us (0.940)
  Pallas kernels: 146 us -> 138 us
    pallas_call x1, Pallas kernels: 146 us -> 138 us  [update_call(): pl.pallas_call(lambda *refs: kernel(n, gain, *refs), out_shape=jax.ShapeD...]
where the time goes in v4:
time: 141 us
  Pallas kernels  138 us (98%)
  other arithmetic  2.28 us (2%)
    pallas_call x1, Pallas kernels, update_call(): pl.pallas_call(lambda *refs: kernel(n, gain, *refs), out_shape=jax.ShapeD...  138 us

profile of v4, /device:TPU:1, one launch (start us, length us, event | category | flops | bytes accessed | tf_op | source)
XLA Modules:
  0.0 141.2 jit_solution(9061548402753913205)
XLA Ops:
  0.6 2.3 %fusion = (bf16[768,256]{1,0:T(8,128)(2,1)S(1)}, f32[768,256]{1,0:T(8,128)}) fusion(bf16[768,256]{1,0:T(8,128)(2,1)} %param.2, f32[768,256]{1,0:T(8,128)} %param.3), kind=kLoop, calls=%fused_computation.2 | loop fusion | flops 1179648 | bytes 2359296 | tf_op jit(solution)/shard_map/convert_element_type | solution.py:722
  2.9 137.5 %shard_map.41 = bf16[768,256]{1,0:T(8,128)(2,1)S(1)} custom-call(bf16[768,256]{1,0:T(8,128)(2,1)S(1)} %get-tuple-element.2.refs_0_), custom_call_target="tpu_custom_call" | custom-call | tf_op jit(solution)/shard_map/pallas_call | solution.py:688
  140.4 0.7 copy.5

commit v5 on v4

--- a/solution.py
+++ b/solution.py
@@ -88,7 +88,7 @@
 
 
 def kernel(
-    n, gain, x_ref, o_ref, xc, part, z1, x1, z2, x2, gram, cube, sums, rpg, cpg, rp2, cp2, rp3, cpp, rph, rpn, cpn, rpw,
+    n, gain, x_ref, o_ref, xc, part, z1, x1, z2, x2, gram, cube, sums, total_ref, rpg, cpg, rp2, cp2, rp3, cpp, rpn, cpn, rpw,
     qi, product, swap, edge, peaks, send_sems, recv_sems, local_sem,
 ):
     nz, nx, nc, ny = n["z"], n["x"], n["c"], n["y"]
@@ -299,7 +299,7 @@
     class Rows:
         def __init__(self, rp):
             self.rp, self.send = rp, comm.send_index()
-            self.near, self.far = comm.recv_index(), {w: comm.recv_index() for w in (1, -1)}
+            self.near, self.rest, self.far = comm.recv_index(), comm.recv_index(), {w: comm.recv_index() for w in (1, -1)}
 
         def to(self, d, way, index, h=None):
             ref = two_halves(self.rp.at[around(z, d, nz)], h, half_rows)
@@ -314,11 +314,15 @@
         def forward(self):
             for w in (1, -1):
                 take(1, self.far[w], "z")
-                self.to(-2 * w, w, self.near)
-                self.to(-2 * w, 2 * w, self.near, 0 if w > 0 else 1)
-
-        def finish(self):
-            take(nz - 3, self.near, "z")
+                self.to(-2 * w, 2 * w, self.rest, 0 if w > 0 else 1)
+                self.to(-2 * w, w, self.rest)
+
+        def finish(self, use=lambda ds: None):
+            use([-2, 2])
+            take(2, self.near, "z")
+            use([-1, 1])
+            take(3, self.rest, "z")
+            use([-3, 3, 4])
 
     class Columns:
         def __init__(self, core, cp):
@@ -386,7 +390,45 @@
         def finish(self):
             take(16, self.over, "c")
 
-    def exchange(rp, cp, half_done=None, rp_next=None, next_piece=None, meanwhile=None, peak=False):
+    def gather_panels(rp, cp, half_done):
+        base_recv, base_send = comm.next_recv, comm.next_send
+        for core in range(nc):
+
+            @pl.when(c == core)
+            def _():
+                comm.next_recv, comm.next_send = base_recv, base_send
+                columns, rows = Columns(core, cp), Rows(rp)
+                columns.begin()
+                rows.begin()
+                columns.spread(0, 0)
+                columns.first()
+                rows.forward()
+                columns.middle()
+                rows.finish()
+                columns.end()
+                half_done()
+                columns.finish()
+                if core == 0:
+                    sent(columns, rows)
+
+        comm.next_recv = comm.most_recv
+
+    def sent(columns, *rows):
+        unsent.append((15, columns.send, "y"))
+        unsent.append((16, columns.send_over, "c"))
+        unsent.extend((7, each.send, "z") for each in rows)
+
+    def adding(left, cp):
+        def use(ds):
+            total = total_ref[...]
+            for d in ds:
+                k = around(z, d, nz)
+                total += jnp.dot(left(k), cp[k // nc, k % nc].reshape(nx * ph, pw), preferred_element_type=F32)
+            total_ref[...] = total
+
+        return use
+
+    def two_products(rp, cp, first, rp_next, next_piece, meanwhile, second, peak=False):
         base_recv, base_send = comm.next_recv, comm.next_send
         for core in range(nc):
 
@@ -395,40 +437,31 @@
                 comm.next_recv, comm.next_send = base_recv, base_send
                 columns, rows = Columns(core, cp), Rows(rp)
                 peak_walk = largest(comm.recv_index()) if peak else iter(())
+                rows.begin()
                 columns.begin()
-                rows.begin()
                 columns.spread(0, 0)
                 next(peak_walk, None)
-                if rp_next is None:
-                    columns.first()
-                    rows.forward()
-                    columns.middle()
-                    rows.finish()
-                    columns.end()
-                    half_done()
-                    columns.finish()
-                else:
-                    rows.forward()
-                    columns.first()
-                    next(peak_walk, None)
-                    rows.finish()
-                    rp_next[z] = next_piece().astype(BF)
-                    next_rows = Rows(rp_next)
-                    next_rows.begin()
-                    columns.middle()
-                    next(peak_walk, None)
-                    next_rows.forward()
-                    columns.end()
-                    next(peak_walk, None)
-                    columns.finish()
-                    meanwhile()
-                    next_rows.finish()
+                total_ref[...] = jnp.zeros(total_ref.shape, F32)
+                first([0])
+                rows.forward()
+                columns.first()
+                next(peak_walk, None)
+                rows.finish(first)
+                rp_next[z] = next_piece(total_ref[...]).astype(BF)
+                next_rows = Rows(rp_next)
+                next_rows.begin()
+                total_ref[...] = jnp.zeros(total_ref.shape, F32)
+                columns.middle()
+                next(peak_walk, None)
+                next_rows.forward()
+                columns.end()
+                next(peak_walk, None)
+                columns.finish()
+                meanwhile()
+                second([0])
+                next_rows.finish(second)
                 if core == 0:
-                    unsent.append((7, rows.send, "z"))
-                    unsent.append((15, columns.send, "y"))
-                    unsent.append((16, columns.send_over, "c"))
-                    if rp_next is not None:
-                        unsent.append((7, next_rows.send, "z"))
+                    sent(columns, rows, next_rows)
 
         comm.next_recv = comm.most_recv
 
@@ -474,7 +507,7 @@
     def first_half():
         (sums[...],) = times([rpg], cpg, c)
 
-    exchange(rpg, cpg, first_half)
+    gather_panels(rpg, cpg, first_half)
 
     def sizes(k, total):
         return total + jnp.abs(rpg[k].astype(F32))
@@ -504,29 +537,27 @@
         lax.fori_loop(0, ny * nc * nx, step, 0)
         cube[...] = mix(gram[...], sums[...], inverse, mine * ph, z * pw)
 
-    exchange(rp2, cp2, None, rp3, lambda: times([rp2], cpg)[0], mixed_columns, peak=True)
-
-    inverse, root = scales()
-
-    def product_rows(k, carry):
+    def rows_of_product(k):
+        inverse, _ = scales()
         once = rpg[k].astype(F32) * inverse
         twice = rp2[k].astype(F32) * inverse * inverse
         thrice = rp3[k].astype(F32) * inverse * inverse * inverse
-        rph[k] = (first_coef * once + second_coef * twice + third_coef * thrice).astype(BF)
-        return carry
-
-    lax.fori_loop(0, nz, product_rows, 0)
-    (next_gram,) = times([rph], cpp)
-    put(next_gram, rpn, cpn)
-
-    def next_first():
-        (value,) = times([rpn], cpp)
+        return (first_coef * once + second_coef * twice + third_coef * thrice).astype(BF)
+
+    two_products(
+        rp2, cp2, adding(lambda k: rp2[k], cpg), rp3, lambda value: value, mixed_columns, adding(rows_of_product, cpp), peak=True
+    )
+    put(total_ref[...], rpn, cpn)
+
+    def next_first(value):
         sums[...] = value
         return value
 
-    exchange(rpn, cpn, None, rpw, next_first, lambda: None)
-    (next_second,) = times([rpw], cpn)
-    whole = (gain * root) * (first_coef * cube[...] + second_coef * sums[...] + third_coef * next_second)
+    two_products(
+        rpn, cpn, adding(lambda k: rpn[k], cpp), rpw, next_first, lambda: None, adding(lambda k: rpw[k], cpn)
+    )
+    _, root = scales()
+    whole = (gain * root) * (first_coef * cube[...] + second_coef * sums[...] + third_coef * total_ref[...])
     qi[z, x] = whole.astype(BF)
 
     def share_of(d):
@@ -700,8 +731,9 @@
             pltpu.VMEM((ph, pw), F32),
             pltpu.VMEM((ph, pw), F32),
             pltpu.VMEM((ph, pw), F32),
+            pltpu.VMEM((ph, pw), F32),
             row_panel, column_panel, row_panel, column_panel, row_panel, column_panel,
-            row_panel, row_panel, column_panel, row_panel,
+            row_panel, column_panel, row_panel,
             pltpu.VMEM((nz, nx, ph, pw), BF),
             pltpu.VMEM((nc, rows_block // nc, columns), F32),
             pltpu.VMEM((2, rows_block // nc, columns), BF),

time: 141 us -> 136 us (0.965)
  Pallas kernels: 138 us -> 132 us
    pallas_call x1, Pallas kernels: 138 us -> 132 us  [update_call(): pl.pallas_call(lambda *refs: kernel(n, gain, *refs), out_shape=jax.ShapeD...]
where the time goes in v5:
time: 136 us
  Pallas kernels  132 us (97%)
  other arithmetic  2.28 us (2%)
    pallas_call x1, Pallas kernels, update_call(): pl.pallas_call(lambda *refs: kernel(n, gain, *refs), out_shape=jax.ShapeD...  132 us

profile of v5, /device:TPU:1, one launch (start us, length us, event | category | flops | bytes accessed | tf_op | source)
XLA Modules:
  0.0 135.8 jit_solution(15369221316810505010)
XLA Ops:
  0.6 2.3 %fusion = (bf16[768,256]{1,0:T(8,128)(2,1)S(1)}, f32[768,256]{1,0:T(8,128)}) fusion(bf16[768,256]{1,0:T(8,128)(2,1)} %param.2, f32[768,256]{1,0:T(8,128)} %param.3), kind=kLoop, calls=%fused_computation.2 | loop fusion | flops 1179648 | bytes 2359296 | tf_op jit(solution)/shard_map/convert_element_type | solution.py:754
  2.9 132.2 %shard_map.41 = bf16[768,256]{1,0:T(8,128)(2,1)S(1)} custom-call(bf16[768,256]{1,0:T(8,128)(2,1)S(1)} %get-tuple-element.2.refs_0_), custom_call_target="tpu_custom_call" | custom-call | tf_op jit(solution)/shard_map/pallas_call | solution.py:719
  135.1 0.7 copy.5

commit v6 on v5

--- a/solution.py
+++ b/solution.py
@@ -504,16 +504,16 @@
 
     put(gram[...], rpg, cpg)
 
+    def sizes(k, total):
+        return total + jnp.abs(rpg[k].astype(F32))
+
     def first_half():
         (sums[...],) = times([rpg], cpg, c)
+        row_sums = jnp.sum(lax.fori_loop(0, nz, sizes, jnp.zeros((ph, pw), F32)), axis=1, keepdims=True)
+        edge[0] = jnp.broadcast_to(jnp.max(row_sums, axis=0, keepdims=True), edge.shape[1:])
+        product[...] = jnp.zeros(product.shape, F32)
 
     gather_panels(rpg, cpg, first_half)
-
-    def sizes(k, total):
-        return total + jnp.abs(rpg[k].astype(F32))
-
-    row_sums = jnp.sum(lax.fori_loop(0, nz, sizes, jnp.zeros((ph, pw), F32)), axis=1, keepdims=True)
-    edge[0] = jnp.broadcast_to(jnp.max(row_sums, axis=0, keepdims=True), edge.shape[1:])
     (square,) = times([rpg], cpg, 1 - c, (sums[...],))
     sums[...] = square
     put(square, rp2, cp2)
@@ -566,7 +566,6 @@
         for side in range(nc):
             product[side] += jnp.dot(left, right_rows(around(c, 1 - side, nc), k), preferred_element_type=F32)
 
-    product[...] = jnp.zeros(product.shape, F32)
     base_recv, base_send = comm.next_recv, comm.next_send
 
     def q(d, e, h=None):

time: 136 us -> 135 us (level)
  no operation moved by 1% of the time
where the time goes in v6:
time: 135 us
  Pallas kernels  131 us (97%)
  other arithmetic  2.28 us (2%)
    pallas_call x1, Pallas kernels, update_call(): pl.pallas_call(lambda *refs: kernel(n, gain, *refs), out_shape=jax.ShapeD...  131 us

profile of v6, /device:TPU:1, one launch (start us, length us, event | category | flops | bytes accessed | tf_op | source)
XLA Modules:
  0.0 134.9 jit_solution(6473384915665726529)
XLA Ops:
  0.6 2.3 %fusion = (bf16[768,256]{1,0:T(8,128)(2,1)S(1)}, f32[768,256]{1,0:T(8,128)}) fusion(bf16[768,256]{1,0:T(8,128)(2,1)} %param.2, f32[768,256]{1,0:T(8,128)} %param.3), kind=kLoop, calls=%fused_computation.2 | loop fusion | flops 1179648 | bytes 2359296 | tf_op jit(solution)/shard_map/convert_element_type | solution.py:753
  2.9 131.2 %shard_map.41 = bf16[768,256]{1,0:T(8,128)(2,1)S(1)} custom-call(bf16[768,256]{1,0:T(8,128)(2,1)S(1)} %get-tuple-element.2.refs_0_), custom_call_target="tpu_custom_call" | custom-call | tf_op jit(solution)/shard_map/pallas_call | solution.py:718
  134.1 0.7 copy.5
